TPU v7x, 32 devices: a whole 2x2x4 slice. The times are simulated.
32 devices in a mesh: dp: 4 (over z), cp: 8 (over y, x, core).
Axes of the slice: x: 2, y: 2, z: 4, core: 2. Of those that a mesh axis runs over, the one named last changes fastest.
Arguments:
- x: bfloat16 [4096, 6144], P(('dp', 'cp')), parts along dimension 0
- k_cache: bfloat16 [65536, 8, 128], P(('dp', 'cp')), parts along dimension 0
- v_cache: bfloat16 [65536, 8, 128], P(('dp', 'cp')), parts along dimension 0
- ln_gain: bfloat16 [6144], replicated
- w_q: bfloat16 [6144, 12288], replicated
- w_k: bfloat16 [6144, 1024], replicated
- w_v: bfloat16 [6144, 1024], replicated
- w_o: bfloat16 [12288, 6144], replicated
- q_gain: bfloat16 [128], replicated
- k_gain: bfloat16 [128], replicated
Outputs:
- output 1: bfloat16 [4096, 6144], P(('dp', 'cp')), parts along dimension 0
- output 2: bfloat16 [4096, 8, 128], P(('dp', 'cp')), parts along dimension 0
- output 3: bfloat16 [4096, 8, 128], P(('dp', 'cp')), parts along dimension 0
There are 4 independent parts. A program takes and returns all parts, laid end to end along the dimension named above; an argument that names none is the same for every part.
All inputs are finite; a program needn't handle non-finite values.
Results may differ from a plain program's by a relative error of at most 0.0105903.
Values are sent between devices in bfloat16 or wider.
A program may use at most 1.5 GiB of HBM per device.

v0:
```python
import jax
import jax.numpy as jnp
from jax import lax
from jax.sharding import PartitionSpec as P

HEAD_DIM = 128
ROPE_THETA = 1.0e6
NORM_EPS = 1.0e-6
MASK_VALUE = -1.0e30


def rms_norm(vals, gain):
    mean_sq = jnp.mean(vals * vals, axis=-1, keepdims=True)
    return vals * lax.rsqrt(mean_sq + NORM_EPS) * gain


def apply_rope(vals, positions):
    half = HEAD_DIM // 2
    inv_freq = ROPE_THETA ** (-jnp.arange(half, dtype=jnp.float32) * (2.0 / HEAD_DIM))
    angles = positions.astype(jnp.float32)[:, None] * inv_freq[None, :]
    cos_tab = jnp.cos(angles)[:, None, :]
    sin_tab = jnp.sin(angles)[:, None, :]
    first = vals[..., :half]
    second = vals[..., half:]
    return jnp.concatenate([first * cos_tab - second * sin_tab, second * cos_tab + first * sin_tab], axis=-1)


def project_rows(x_wide, ln_gain, w_q, w_k, w_v, q_gain, k_gain, positions):
    rows = x_wide.shape[0]
    hidden = rms_norm(x_wide, ln_gain.astype(jnp.float32)).astype(jnp.bfloat16)
    q_raw = jnp.dot(hidden, w_q, preferred_element_type=jnp.float32).astype(jnp.bfloat16).reshape(rows, -1, HEAD_DIM)
    k_raw = jnp.dot(hidden, w_k, preferred_element_type=jnp.float32).astype(jnp.bfloat16).reshape(rows, -1, HEAD_DIM)
    v_new = jnp.dot(hidden, w_v, preferred_element_type=jnp.float32).astype(jnp.bfloat16).reshape(rows, -1, HEAD_DIM)
    q_rot = apply_rope(rms_norm(q_raw.astype(jnp.float32), q_gain.astype(jnp.float32)), positions).astype(jnp.bfloat16)
    k_new = apply_rope(rms_norm(k_raw.astype(jnp.float32), k_gain.astype(jnp.float32)), positions).astype(jnp.bfloat16)
    return q_rot, k_new, v_new


def partial_attend(q_grp, keys, vals, allowed):
    scale = HEAD_DIM ** -0.5
    scores = jnp.einsum('rkgd,skd->krgs', q_grp, keys, preferred_element_type=jnp.float32) * scale
    if allowed is not None:
        scores = jnp.where(allowed[None, :, None, :], scores, MASK_VALUE)
    peak = jnp.max(scores, axis=-1)
    weights = jnp.exp(scores - peak[..., None])
    weighted = jnp.einsum('krgs,skd->krgd', weights.astype(jnp.bfloat16), vals, preferred_element_type=jnp.float32)
    return peak, jnp.sum(weights, axis=-1), weighted


def combine_two(first, second):
    peak_a, sum_a, acc_a = first
    peak_b, sum_b, acc_b = second
    top_peak = jnp.maximum(jnp.max(peak_a, axis=0), jnp.max(peak_b, axis=0))
    factor_a = jnp.exp(peak_a - top_peak[None])
    factor_b = jnp.exp(peak_b - top_peak[None])
    total_sum = jnp.sum(factor_a * sum_a, axis=0) + jnp.sum(factor_b * sum_b, axis=0)
    total = jnp.sum(factor_a[..., None] * acc_a, axis=0) + jnp.sum(factor_b[..., None] * acc_b, axis=0)
    return total / total_sum[..., None]


def solution(mesh):
    cp_size = mesh.shape['cp']
    row_spec = P(('dp', 'cp'), None)
    cache_spec = P(('dp', 'cp'), None, None)
    whole = P()

    def device_step(x_rows, k_cache, v_cache, ln_gain, w_q, w_k, w_v, w_o, q_gain, k_gain):
        rows = x_rows.shape[0]
        prefix_len = k_cache.shape[0] * cp_size
        kv_heads = k_cache.shape[1]
        q_heads = w_q.shape[1] // HEAD_DIM
        group = q_heads // kv_heads
        my_index = lax.axis_index('cp')
        row_ids = my_index * rows + jnp.arange(rows)
        key_ids = jnp.arange(rows)
        x_wide = x_rows.astype(jnp.float32)
        q_rot, k_new, v_new = project_rows(x_wide, ln_gain, w_q, w_k, w_v, q_gain, k_gain, prefix_len + row_ids)
        q_grp = q_rot.reshape(rows, kv_heads, group, HEAD_DIM)
        every_q = lax.all_gather(q_grp, 'cp')
        every_k = lax.all_gather(k_new, 'cp')
        every_v = lax.all_gather(v_new, 'cp')

        def block_work(block):
            q_block, k_block, v_block, source = block
            prefix_part = partial_attend(q_block, k_cache, v_cache, None)
            allowed = (source * rows + key_ids)[None, :] <= row_ids[:, None]
            new_part = partial_attend(q_grp, k_block, v_block, allowed)
            return prefix_part, new_part

        prefix_parts, new_parts = lax.map(block_work, (every_q, every_k, every_v, jnp.arange(cp_size)))
        returned = tuple(lax.all_to_all(piece, 'cp', 0, 0, tiled=True) for piece in prefix_parts)
        attended = combine_two(returned, new_parts)
        attended = jnp.transpose(attended, (1, 0, 2, 3)).reshape(rows, q_heads * HEAD_DIM).astype(jnp.bfloat16)
        out = (x_wide + jnp.dot(attended, w_o, preferred_element_type=jnp.float32)).astype(jnp.bfloat16)
        return out, k_new, v_new

    return jax.shard_map(device_step, mesh=mesh, in_specs=(row_spec, cache_spec, cache_spec, whole, whole, whole, whole, whole, whole, whole), out_specs=(row_spec, cache_spec, cache_spec), check_vma=False)
```

profile of v0, /device:TPU:0, one launch (start us, length us, event | category | flops | bytes accessed | tf_op | source)
XLA Modules:
  0.0 1844.3 jit_solution(14352774931931754125)
XLA Ops:
  9.7 7.0 fusion.39
  18.0 6.4 fusion.38
  27.4 49.8 %fusion.36 = f32[16,8,96,128]{3,1,2,0:T(8,128)} fusion(bf16[6144,12288]{1,0:T(8,128)(2,1)} %param.16, bf16[128,6144]{1,0:T(8,128)(2,1)S(1)} %copy-done.3, f32[6144]{0:T(1024)S(1)} %convert_element_type.77, f32[128]{0:T(128)S(1)} %add_rsqrt_fusion.2), kind=kOutput, calls=%fused_computation.58 | convolution fusion | flops 19333644288 | bytes 158884352 | tf_op jit(solution)/shard_map/dot_general | solution.py:31
  77.2 6.5 copy.183
  83.8 6.6 copy.140
  90.3 5.0 multiply_reduce_fusion.3
  95.5 4.0 multiply_multiply_fusion
  102.4 4.9 copy.141
  107.4 4.8 copy.149
  112.3 2.7 copy.150
  114.9 2.8 copy.147
  117.7 2.8 copy.146
  120.4 4.6 pad_maximum_fusion.1
  125.1 110.4 %all-gather.4.cloned.1.call-done = bf16[8,128,8,12,128]{4,2,3,1,0:T(8,128)(2,1)} async-done(((bf16[1,128,8,12,128]{4,2,3,1,0:T(8,128)(2,1)}), bf16[8,128,8,12,128]{4,2,3,1,0:T(8,128)(2,1)}) %all-gather.4.cloned.1.call-update) | async-done | bytes 25165840 | tf_op jit(solution)/shard_map/all_gather | solution.py:79
  235.5 943.6 %while.21 = (s32[]{:T(128)}, f32[8,8,128,12]{2,1,3,0:T(8,128)}, f32[8,8,128,12]{2,1,3,0:T(8,128)}, f32[8,8,128,12,128]{4,2,3,1,0:T(8,128)}, f32[8,8,128,12]{2,3,...) while((s32[]{:T(128)}, f32[8,8,128,12]{2,1,3,0:T(8,128)}, ...), condition=%wide.region_8.9_spmd.clone, body=%wide.region_3.8_spmd.clone.sunk | while | flops 13908803584 | bytes 398805248 | solution.py:90
  239.1 2.1 constant_dynamic-slice_fusion.6
  244.9 4.3 bitcast_dynamic-update-slice_fusion.8
  249.3 34.5 %multiply_reduce_fusion.8 = (f32[8,128,12]{1,2,0:T(8,128)S(1)}, f32[8,128,12,2048]{3,1,2,0:T(8,128)}) fusion(bf16[2048,8,128]{2,0,1:T(8,128)(2,1)S(1)} %copy-done, bf16[1,128,8,12,128]{4,2,3,1,0:T(8,128)(2,1)S(1)} %constant_dynamic-slice_fusion.6), kind=kOutput, calls=%fused_computation.3.clone.1 | convolution fusion | flops 6492770304 | bytes 108052480 | tf_op jit(solution)/shard_map/while/body/eval_jaxpr/rkgd,skd->krgs/dot_general | solution.py:41
  283.7 31.1 %fusion.67 = f32[8,128,12]{1,2,0:T(8,128)S(1)} fusion(f32[8,128,12,2048]{3,1,2,0:T(8,128)} %get-tuple-element.398, f32[8,128,12]{1,2,0:T(8,128)S(1)} %get-tuple-element.395), kind=kLoop, calls=%fused_computation.5.clone.1 | loop fusion | flops 75485184 | bytes 100761600 | tf_op jit(solution)/shard_map/while/body/eval_jaxpr/reduce_sum | solution.py:47
  314.9 37.4 %bitcast_dynamic-update-slice_fusion.6 = f32[8,8,128,12,128]{4,2,3,1,0:T(8,128)} fusion(f32[8,8,128,12,128]{4,2,3,1,0:T(8,128)} %get-tuple-element.421, s32[]{:T(128)S(6)} %copy.228, bf16[2048,8,128]{2,0,1:T(8,128)(2,1)} %get-tuple-element.444, f32[8,128,12,2048]{3,1,2,0:T(8,128)} %get-tuple-element.398, f32[8,128,12]{1,2,0:T(8,128)S(1)} %get-tuple-element.395), kind=kOutput, calls=%fused_computation.9.clone.1 | convolution fusion | flops 6517948416 | bytes 111198208 | tf_op jit(solution)/shard_map/while/body/eval_jaxpr/krgs,skd->krgd/dot_general | solution.py:46
  357.0 2.1 constant_dynamic-slice_fusion.6
  362.8 4.3 bitcast_dynamic-update-slice_fusion.8
  367.2 34.5 %multiply_reduce_fusion.8 = (f32[8,128,12]{1,2,0:T(8,128)S(1)}, f32[8,128,12,2048]{3,1,2,0:T(8,128)}) fusion(bf16[2048,8,128]{2,0,1:T(8,128)(2,1)S(1)} %copy-done, bf16[1,128,8,12,128]{4,2,3,1,0:T(8,128)(2,1)S(1)} %constant_dynamic-slice_fusion.6), kind=kOutput, calls=%fused_computation.3.clone.1 | convolution fusion | flops 6492770304 | bytes 108052480 | tf_op jit(solution)/shard_map/while/body/eval_jaxpr/rkgd,skd->krgs/dot_general | solution.py:41
  401.7 31.1 %fusion.67 = f32[8,128,12]{1,2,0:T(8,128)S(1)} fusion(f32[8,128,12,2048]{3,1,2,0:T(8,128)} %get-tuple-element.398, f32[8,128,12]{1,2,0:T(8,128)S(1)} %get-tuple-element.395), kind=kLoop, calls=%fused_computation.5.clone.1 | loop fusion | flops 75485184 | bytes 100761600 | tf_op jit(solution)/shard_map/while/body/eval_jaxpr/reduce_sum | solution.py:47
  432.8 37.4 %bitcast_dynamic-update-slice_fusion.6 = f32[8,8,128,12,128]{4,2,3,1,0:T(8,128)} fusion(f32[8,8,128,12,128]{4,2,3,1,0:T(8,128)} %get-tuple-element.421, s32[]{:T(128)S(6)} %copy.228, bf16[2048,8,128]{2,0,1:T(8,128)(2,1)} %get-tuple-element.444, f32[8,128,12,2048]{3,1,2,0:T(8,128)} %get-tuple-element.398, f32[8,128,12]{1,2,0:T(8,128)S(1)} %get-tuple-element.395), kind=kOutput, calls=%fused_computation.9.clone.1 | convolution fusion | flops 6517948416 | bytes 111198208 | tf_op jit(solution)/shard_map/while/body/eval_jaxpr/krgs,skd->krgd/dot_general | solution.py:46
  474.9 2.1 constant_dynamic-slice_fusion.6
  480.7 4.3 bitcast_dynamic-update-slice_fusion.8
  485.1 34.5 %multiply_reduce_fusion.8 = (f32[8,128,12]{1,2,0:T(8,128)S(1)}, f32[8,128,12,2048]{3,1,2,0:T(8,128)}) fusion(bf16[2048,8,128]{2,0,1:T(8,128)(2,1)S(1)} %copy-done, bf16[1,128,8,12,128]{4,2,3,1,0:T(8,128)(2,1)S(1)} %constant_dynamic-slice_fusion.6), kind=kOutput, calls=%fused_computation.3.clone.1 | convolution fusion | flops 6492770304 | bytes 108052480 | tf_op jit(solution)/shard_map/while/body/eval_jaxpr/rkgd,skd->krgs/dot_general | solution.py:41
  519.5 31.1 %fusion.67 = f32[8,128,12]{1,2,0:T(8,128)S(1)} fusion(f32[8,128,12,2048]{3,1,2,0:T(8,128)} %get-tuple-element.398, f32[8,128,12]{1,2,0:T(8,128)S(1)} %get-tuple-element.395), kind=kLoop, calls=%fused_computation.5.clone.1 | loop fusion | flops 75485184 | bytes 100761600 | tf_op jit(solution)/shard_map/while/body/eval_jaxpr/reduce_sum | solution.py:47
  550.7 37.4 %bitcast_dynamic-update-slice_fusion.6 = f32[8,8,128,12,128]{4,2,3,1,0:T(8,128)} fusion(f32[8,8,128,12,128]{4,2,3,1,0:T(8,128)} %get-tuple-element.421, s32[]{:T(128)S(6)} %copy.228, bf16[2048,8,128]{2,0,1:T(8,128)(2,1)} %get-tuple-element.444, f32[8,128,12,2048]{3,1,2,0:T(8,128)} %get-tuple-element.398, f32[8,128,12]{1,2,0:T(8,128)S(1)} %get-tuple-element.395), kind=kOutput, calls=%fused_computation.9.clone.1 | convolution fusion | flops 6517948416 | bytes 111198208 | tf_op jit(solution)/shard_map/while/body/eval_jaxpr/krgs,skd->krgd/dot_general | solution.py:46
  592.8 2.1 constant_dynamic-slice_fusion.6
  598.6 4.2 bitcast_dynamic-update-slice_fusion.8
  602.9 34.5 %multiply_reduce_fusion.8 = (f32[8,128,12]{1,2,0:T(8,128)S(1)}, f32[8,128,12,2048]{3,1,2,0:T(8,128)}) fusion(bf16[2048,8,128]{2,0,1:T(8,128)(2,1)S(1)} %copy-done, bf16[1,128,8,12,128]{4,2,3,1,0:T(8,128)(2,1)S(1)} %constant_dynamic-slice_fusion.6), kind=kOutput, calls=%fused_computation.3.clone.1 | convolution fusion | flops 6492770304 | bytes 108052480 | tf_op jit(solution)/shard_map/while/body/eval_jaxpr/rkgd,skd->krgs/dot_general | solution.py:41
  637.4 31.1 %fusion.67 = f32[8,128,12]{1,2,0:T(8,128)S(1)} fusion(f32[8,128,12,2048]{3,1,2,0:T(8,128)} %get-tuple-element.398, f32[8,128,12]{1,2,0:T(8,128)S(1)} %get-tuple-element.395), kind=kLoop, calls=%fused_computation.5.clone.1 | loop fusion | flops 75485184 | bytes 100761600 | tf_op jit(solution)/shard_map/while/body/eval_jaxpr/reduce_sum | solution.py:47
  668.5 37.4 %bitcast_dynamic-update-slice_fusion.6 = f32[8,8,128,12,128]{4,2,3,1,0:T(8,128)} fusion(f32[8,8,128,12,128]{4,2,3,1,0:T(8,128)} %get-tuple-element.421, s32[]{:T(128)S(6)} %copy.228, bf16[2048,8,128]{2,0,1:T(8,128)(2,1)} %get-tuple-element.444, f32[8,128,12,2048]{3,1,2,0:T(8,128)} %get-tuple-element.398, f32[8,128,12]{1,2,0:T(8,128)S(1)} %get-tuple-element.395), kind=kOutput, calls=%fused_computation.9.clone.1 | convolution fusion | flops 6517948416 | bytes 111198208 | tf_op jit(solution)/shard_map/while/body/eval_jaxpr/krgs,skd->krgd/dot_general | solution.py:46
  710.7 2.1 constant_dynamic-slice_fusion.6
  716.5 4.4 bitcast_dynamic-update-slice_fusion.8
  720.9 34.5 %multiply_reduce_fusion.8 = (f32[8,128,12]{1,2,0:T(8,128)S(1)}, f32[8,128,12,2048]{3,1,2,0:T(8,128)}) fusion(bf16[2048,8,128]{2,0,1:T(8,128)(2,1)S(1)} %copy-done, bf16[1,128,8,12,128]{4,2,3,1,0:T(8,128)(2,1)S(1)} %constant_dynamic-slice_fusion.6), kind=kOutput, calls=%fused_computation.3.clone.1 | convolution fusion | flops 6492770304 | bytes 108052480 | tf_op jit(solution)/shard_map/while/body/eval_jaxpr/rkgd,skd->krgs/dot_general | solution.py:41
  755.3 31.1 %fusion.67 = f32[8,128,12]{1,2,0:T(8,128)S(1)} fusion(f32[8,128,12,2048]{3,1,2,0:T(8,128)} %get-tuple-element.398, f32[8,128,12]{1,2,0:T(8,128)S(1)} %get-tuple-element.395), kind=kLoop, calls=%fused_computation.5.clone.1 | loop fusion | flops 75485184 | bytes 100761600 | tf_op jit(solution)/shard_map/while/body/eval_jaxpr/reduce_sum | solution.py:47
  786.5 37.4 %bitcast_dynamic-update-slice_fusion.6 = f32[8,8,128,12,128]{4,2,3,1,0:T(8,128)} fusion(f32[8,8,128,12,128]{4,2,3,1,0:T(8,128)} %get-tuple-element.421, s32[]{:T(128)S(6)} %copy.228, bf16[2048,8,128]{2,0,1:T(8,128)(2,1)} %get-tuple-element.444, f32[8,128,12,2048]{3,1,2,0:T(8,128)} %get-tuple-element.398, f32[8,128,12]{1,2,0:T(8,128)S(1)} %get-tuple-element.395), kind=kOutput, calls=%fused_computation.9.clone.1 | convolution fusion | flops 6517948416 | bytes 111198208 | tf_op jit(solution)/shard_map/while/body/eval_jaxpr/krgs,skd->krgd/dot_general | solution.py:46
  828.6 2.1 constant_dynamic-slice_fusion.6
  834.4 4.3 bitcast_dynamic-update-slice_fusion.8
  838.8 34.5 %multiply_reduce_fusion.8 = (f32[8,128,12]{1,2,0:T(8,128)S(1)}, f32[8,128,12,2048]{3,1,2,0:T(8,128)}) fusion(bf16[2048,8,128]{2,0,1:T(8,128)(2,1)S(1)} %copy-done, bf16[1,128,8,12,128]{4,2,3,1,0:T(8,128)(2,1)S(1)} %constant_dynamic-slice_fusion.6), kind=kOutput, calls=%fused_computation.3.clone.1 | convolution fusion | flops 6492770304 | bytes 108052480 | tf_op jit(solution)/shard_map/while/body/eval_jaxpr/rkgd,skd->krgs/dot_general | solution.py:41
  873.3 31.1 %fusion.67 = f32[8,128,12]{1,2,0:T(8,128)S(1)} fusion(f32[8,128,12,2048]{3,1,2,0:T(8,128)} %get-tuple-element.398, f32[8,128,12]{1,2,0:T(8,128)S(1)} %get-tuple-element.395), kind=kLoop, calls=%fused_computation.5.clone.1 | loop fusion | flops 75485184 | bytes 100761600 | tf_op jit(solution)/shard_map/while/body/eval_jaxpr/reduce_sum | solution.py:47
  904.4 37.4 %bitcast_dynamic-update-slice_fusion.6 = f32[8,8,128,12,128]{4,2,3,1,0:T(8,128)} fusion(f32[8,8,128,12,128]{4,2,3,1,0:T(8,128)} %get-tuple-element.421, s32[]{:T(128)S(6)} %copy.228, bf16[2048,8,128]{2,0,1:T(8,128)(2,1)} %get-tuple-element.444, f32[8,128,12,2048]{3,1,2,0:T(8,128)} %get-tuple-element.398, f32[8,128,12]{1,2,0:T(8,128)S(1)} %get-tuple-element.395), kind=kOutput, calls=%fused_computation.9.clone.1 | convolution fusion | flops 6517948416 | bytes 111198208 | tf_op jit(solution)/shard_map/while/body/eval_jaxpr/krgs,skd->krgd/dot_general | solution.py:46
  946.6 2.1 constant_dynamic-slice_fusion.6
  952.3 4.3 bitcast_dynamic-update-slice_fusion.8
  956.7 34.5 %multiply_reduce_fusion.8 = (f32[8,128,12]{1,2,0:T(8,128)S(1)}, f32[8,128,12,2048]{3,1,2,0:T(8,128)}) fusion(bf16[2048,8,128]{2,0,1:T(8,128)(2,1)S(1)} %copy-done, bf16[1,128,8,12,128]{4,2,3,1,0:T(8,128)(2,1)S(1)} %constant_dynamic-slice_fusion.6), kind=kOutput, calls=%fused_computation.3.clone.1 | convolution fusion | flops 6492770304 | bytes 108052480 | tf_op jit(solution)/shard_map/while/body/eval_jaxpr/rkgd,skd->krgs/dot_general | solution.py:41
  991.1 31.1 %fusion.67 = f32[8,128,12]{1,2,0:T(8,128)S(1)} fusion(f32[8,128,12,2048]{3,1,2,0:T(8,128)} %get-tuple-element.398, f32[8,128,12]{1,2,0:T(8,128)S(1)} %get-tuple-element.395), kind=kLoop, calls=%fused_computation.5.clone.1 | loop fusion | flops 75485184 | bytes 100761600 | tf_op jit(solution)/shard_map/while/body/eval_jaxpr/reduce_sum | solution.py:47
  1022.3 37.4 %bitcast_dynamic-update-slice_fusion.6 = f32[8,8,128,12,128]{4,2,3,1,0:T(8,128)} fusion(f32[8,8,128,12,128]{4,2,3,1,0:T(8,128)} %get-tuple-element.421, s32[]{:T(128)S(6)} %copy.228, bf16[2048,8,128]{2,0,1:T(8,128)(2,1)} %get-tuple-element.444, f32[8,128,12,2048]{3,1,2,0:T(8,128)} %get-tuple-element.398, f32[8,128,12]{1,2,0:T(8,128)S(1)} %get-tuple-element.395), kind=kOutput, calls=%fused_computation.9.clone.1 | convolution fusion | flops 6517948416 | bytes 111198208 | tf_op jit(solution)/shard_map/while/body/eval_jaxpr/krgs,skd->krgd/dot_general | solution.py:46
  1064.5 2.1 constant_dynamic-slice_fusion.6
  1070.2 4.2 bitcast_dynamic-update-slice_fusion.8
  1074.5 34.5 %multiply_reduce_fusion.8 = (f32[8,128,12]{1,2,0:T(8,128)S(1)}, f32[8,128,12,2048]{3,1,2,0:T(8,128)}) fusion(bf16[2048,8,128]{2,0,1:T(8,128)(2,1)S(1)} %copy-done, bf16[1,128,8,12,128]{4,2,3,1,0:T(8,128)(2,1)S(1)} %constant_dynamic-slice_fusion.6), kind=kOutput, calls=%fused_computation.3.clone.1 | convolution fusion | flops 6492770304 | bytes 108052480 | tf_op jit(solution)/shard_map/while/body/eval_jaxpr/rkgd,skd->krgs/dot_general | solution.py:41
  1109.0 31.1 %fusion.67 = f32[8,128,12]{1,2,0:T(8,128)S(1)} fusion(f32[8,128,12,2048]{3,1,2,0:T(8,128)} %get-tuple-element.398, f32[8,128,12]{1,2,0:T(8,128)S(1)} %get-tuple-element.395), kind=kLoop, calls=%fused_computation.5.clone.1 | loop fusion | flops 75485184 | bytes 100761600 | tf_op jit(solution)/shard_map/while/body/eval_jaxpr/reduce_sum | solution.py:47
  1140.1 37.4 %bitcast_dynamic-update-slice_fusion.6 = f32[8,8,128,12,128]{4,2,3,1,0:T(8,128)} fusion(f32[8,8,128,12,128]{4,2,3,1,0:T(8,128)} %get-tuple-element.421, s32[]{:T(128)S(6)} %copy.228, bf16[2048,8,128]{2,0,1:T(8,128)(2,1)} %get-tuple-element.444, f32[8,128,12,2048]{3,1,2,0:T(8,128)} %get-tuple-element.398, f32[8,128,12]{1,2,0:T(8,128)S(1)} %get-tuple-element.395), kind=kOutput, calls=%fused_computation.9.clone.1 | convolution fusion | flops 6517948416 | bytes 111198208 | tf_op jit(solution)/shard_map/while/body/eval_jaxpr/krgs,skd->krgd/dot_general | solution.py:46
  1179.1 11.5 all_to_all.15
  1190.6 11.5 all_to_all.16
  1202.0 8.7 all-to-all-start.1
  1214.2 20.0 %multiply_reduce_fusion.1 = f32[8,128,12,128]{3,1,2,0:T(8,128)} fusion(f32[8,8,128,12,128]{4,2,3,1,0:T(8,128)} %get-tuple-element.93, f32[8,8,128,12]{2,3,1,0:T(8,128)S(1)} %copy.157), kind=kLoop, calls=%fused_computation.39 | loop fusion | flops 23592960 | bytes 57016320 | tf_op jit(solution)/shard_map/reduce_sum | solution.py:57
  1234.2 520.3 %all-to-all-done.1 = f32[8,8,128,12,128]{4,2,3,1,0:T(8,128)} async-done(((f32[8,8,128,12,128]{4,2,3,1,0:T(8,128)}), f32[8,8,128,12,128]{4,2,3,1,0:T(8,128)}, u32[]{:S(2)}, u32[]{:S(2)}) %all-to-all-start.1) | async-done | bytes 50331680 | tf_op jit(solution)/shard_map/all_to_all | solution.py:91
  1754.5 20.0 %multiply_reduce_fusion.2 = f32[8,128,12,128]{3,1,2,0:T(8,128)} fusion(f32[8,8,128,12,128]{4,2,3,1,0:T(8,128)} %all-to-all-done.1, f32[8,8,128,12]{2,3,1,0:T(8,128)S(1)} %copy.155), kind=kLoop, calls=%fused_computation.40 | loop fusion | flops 23592960 | bytes 57016320 | tf_op jit(solution)/shard_map/reduce_sum | solution.py:57
  1774.6 7.7 fusion.32
  1782.2 4.8 copy.161
  1787.1 50.2 %fusion.31 = bf16[128,6144]{1,0:T(8,128)(2,1)} fusion(bf16[128,12288]{0,1:T(8,128)(2,1)} %bitcast.127, bf16[12288,6144]{1,0:T(8,128)(2,1)} %param.19, bf16[128,6144]{1,0:T(8,128)(2,1)S(1)} %copy-done.4), kind=kOutput, calls=%fused_computation.44 | convolution fusion | flops 19329712128 | bytes 157286400 | tf_op jit(solution)/shard_map/dot_general | solution.py:94
  (203 shorter events, 74.7 us)
Async XLA Ops:
  7.2 117.9 %all-gather.8.cloned.1.call-start = ((), (), s32[]{:S(2)}) async-start(), calls=%async_computation.5 | async-start | bytes 2359296 | tf_op jit(solution)/shard_map/all_gather | solution.py:81
  9.7 7.8 copy-start.11
  9.7 8.3 copy-start.3
  17.5 107.5 %all-gather.6.cloned.1.call-start = ((), (), s32[]{:S(2)}) async-start(), calls=%async_computation.4 | async-start | bytes 2359296 | tf_op jit(solution)/shard_map/all_gather | solution.py:80
  25.5 0.7 copy-start.6
  25.5 0.8 copy-start.8
  27.2 50.1 %copy-start.12 = (bf16[128]{0:T(256)(128)(2,1)S(1)}, bf16[128]{0:T(256)(128)(2,1)}, u32[]{:S(2)}) copy-start(bf16[128]{0:T(256)(128)(2,1)} %param.20) | copy-start | bytes 772
  27.2 208.3 %all-gather.4.cloned.1.call-start = ((), (), s32[]{:S(2)}) async-start(), calls=%async_computation.3 | async-start | bytes 28311552 | tf_op jit(solution)/shard_map/all_gather | solution.py:79
  107.4 4.8 copy-start.5
  235.7 6.7 copy-start.1
  244.9 4.3 copy-start
  314.9 38.7 %copy-start.2 = (bf16[128,8,12,128]{3,0,2,1:T(8,128)(2,1)S(1)}, bf16[128,8,12,128]{3,0,2,1:T(8,128)(2,1)}, u32[]{:S(2)}) copy-start(bf16[128,8,12,128]{3,0,2,1:T(8,128)(2,1)} %copy-done.1) | copy-start | bytes 9437188 | tf_op jit(solution)/shard_map/while
  353.6 6.7 copy-start.1
  362.8 4.3 copy-start
  432.8 38.7 %copy-start.2 = (bf16[128,8,12,128]{3,0,2,1:T(8,128)(2,1)S(1)}, bf16[128,8,12,128]{3,0,2,1:T(8,128)(2,1)}, u32[]{:S(2)}) copy-start(bf16[128,8,12,128]{3,0,2,1:T(8,128)(2,1)} %copy-done.1) | copy-start | bytes 9437188 | tf_op jit(solution)/shard_map/while
  471.5 6.7 copy-start.1
  480.7 4.3 copy-start
  550.7 38.7 %copy-start.2 = (bf16[128,8,12,128]{3,0,2,1:T(8,128)(2,1)S(1)}, bf16[128,8,12,128]{3,0,2,1:T(8,128)(2,1)}, u32[]{:S(2)}) copy-start(bf16[128,8,12,128]{3,0,2,1:T(8,128)(2,1)} %copy-done.1) | copy-start | bytes 9437188 | tf_op jit(solution)/shard_map/while
  589.4 6.7 copy-start.1
  598.6 4.2 copy-start
  668.5 38.7 %copy-start.2 = (bf16[128,8,12,128]{3,0,2,1:T(8,128)(2,1)S(1)}, bf16[128,8,12,128]{3,0,2,1:T(8,128)(2,1)}, u32[]{:S(2)}) copy-start(bf16[128,8,12,128]{3,0,2,1:T(8,128)(2,1)} %copy-done.1) | copy-start | bytes 9437188 | tf_op jit(solution)/shard_map/while
  707.2 6.7 copy-start.1
  716.5 4.4 copy-start
  786.5 38.7 %copy-start.2 = (bf16[128,8,12,128]{3,0,2,1:T(8,128)(2,1)S(1)}, bf16[128,8,12,128]{3,0,2,1:T(8,128)(2,1)}, u32[]{:S(2)}) copy-start(bf16[128,8,12,128]{3,0,2,1:T(8,128)(2,1)} %copy-done.1) | copy-start | bytes 9437188 | tf_op jit(solution)/shard_map/while
  825.2 6.7 copy-start.1
  834.4 4.3 copy-start
  904.4 38.8 %copy-start.2 = (bf16[128,8,12,128]{3,0,2,1:T(8,128)(2,1)S(1)}, bf16[128,8,12,128]{3,0,2,1:T(8,128)(2,1)}, u32[]{:S(2)}) copy-start(bf16[128,8,12,128]{3,0,2,1:T(8,128)(2,1)} %copy-done.1) | copy-start | bytes 9437188 | tf_op jit(solution)/shard_map/while
  943.2 6.7 copy-start.1
  952.3 4.3 copy-start
  1022.3 38.7 %copy-start.2 = (bf16[128,8,12,128]{3,0,2,1:T(8,128)(2,1)S(1)}, bf16[128,8,12,128]{3,0,2,1:T(8,128)(2,1)}, u32[]{:S(2)}) copy-start(bf16[128,8,12,128]{3,0,2,1:T(8,128)(2,1)} %copy-done.1) | copy-start | bytes 9437188 | tf_op jit(solution)/shard_map/while
  1061.0 6.7 copy-start.1
  1070.2 4.2 copy-start
  1140.1 38.7 %copy-start.2 = (bf16[128,8,12,128]{3,0,2,1:T(8,128)(2,1)S(1)}, bf16[128,8,12,128]{3,0,2,1:T(8,128)(2,1)}, u32[]{:S(2)}) copy-start(bf16[128,8,12,128]{3,0,2,1:T(8,128)(2,1)} %copy-done.1) | copy-start | bytes 9437188 | tf_op jit(solution)/shard_map/while
  1202.0 8.7 copy-start.7
  1202.0 8.7 copy-start.9
  1202.0 10.7 copy-start.10
  1202.0 552.5 %all-to-all-start.1 = ((f32[8,8,128,12,128]{4,2,3,1,0:T(8,128)}), f32[8,8,128,12,128]{4,2,3,1,0:T(8,128)}, u32[]{:S(2)}, u32[]{:S(2)}) async-start(f32[8,8,128,12,128]{4,2,3,1,0:T(8,128)} %get-tuple-element.92), calls=%async_computation.1 | async-start | bytes 100663296 | tf_op jit(solution)/shard_map/all_to_all | solution.py:91
  1782.2 4.8 copy-start.4
Sparse Core Ops, SparseCore 0:
  17.6 30.2 all-gather.7
  50.4 27.4 all-gather.5
  107.5 127.9 all-gather.3
where the time goes:
time: 1850 us; the launch traced here: 1840 us
  matrix products  733 us (40%)
  waiting for transfers between devices  631 us (34%)
  other arithmetic  336 us (18%)
  local copies, waits for them, and re-layouts  91.4 us (5%)
  blocking collectives  22.9 us (1%)
    all_to_all x1, waiting for transfers between devices, device_step(): lax.all_to_all(piece, 'cp', 0, 0, tiled=True)  520 us
    dot_general x16, matrix products, partial_attend(): jnp.einsum('krgs,skd->krgd', weights.astype(jnp.bfloat16), vals, preferre...  334 us
    dot_general x16, matrix products, partial_attend(): jnp.einsum('rkgd,skd->krgs', q_grp, keys, preferred_element_type=jnp.floa...  285 us
    reduce_sum x16, other arithmetic, partial_attend(): return (peak, jnp.sum(weights, axis=-1), weighted)  264 us
    all_gather x1, waiting for transfers between devices, device_step(): every_q = lax.all_gather(q_grp, 'cp')  110 us
    dot_general x1, matrix products, device_step(): jnp.dot(attended, w_o, preferred_element_type=jnp.float32)  50.2 us
    dot_general x1, matrix products, project_rows(): jnp.dot(hidden, w_q, preferred_element_type=jnp.float32)  49.8 us
    dynamic_slice x32, local copies, waits for them, and re-layouts, device_step(): lax.map(block_work, (every_q, every_k, every_v, jnp.arange(cp_size)))  37.7 us
  transfers between devices with their start and end apart: 4, of which 2 were waited for; matrix products, arithmetic and copies ran while one was open for 7% of the time, Pallas kernels for 0%

commit v1 on v0

v1 whole, which is shorter than its diff:
```python
import functools
import math

import jax
import jax.numpy as jnp
from jax import lax
from jax.experimental import pallas as pl
from jax.experimental.pallas import tpu as pltpu
from jax.sharding import PartitionSpec as P

HEAD_DIM = 128
ROPE_THETA = 1.0e6
NORM_EPS = 1.0e-6
MESH = pl.DeviceIdType.MESH
F32 = jnp.float32
BF16 = jnp.bfloat16

ORD = (0, 1, 2, 4, 3, 5, 6, 7)
SUB = 256
HEADS_PER_TILE = 4


def rms_norm(vals, gain):
    mean_sq = jnp.mean(vals * vals, axis=-1, keepdims=True)
    return vals * lax.rsqrt(mean_sq + NORM_EPS) * gain


def apply_rope(vals, positions):
    half = HEAD_DIM // 2
    inv_freq = ROPE_THETA ** (-jnp.arange(half, dtype=F32) * (2.0 / HEAD_DIM))
    angles = positions.astype(F32)[:, None] * inv_freq[None, :]
    cos_tab = jnp.cos(angles)[:, None, :]
    sin_tab = jnp.sin(angles)[:, None, :]
    first = vals[..., :half]
    second = vals[..., half:]
    return jnp.concatenate([first * cos_tab - second * sin_tab, second * cos_tab + first * sin_tab], axis=-1)


def project_rows(x_wide, ln_gain, w_q, w_k, w_v, q_gain, k_gain, positions):
    rows = x_wide.shape[0]
    hidden = rms_norm(x_wide, ln_gain.astype(F32)).astype(BF16)
    q_raw = jnp.dot(hidden, w_q, preferred_element_type=F32).astype(BF16).reshape(rows, -1, HEAD_DIM)
    k_raw = jnp.dot(hidden, w_k, preferred_element_type=F32).astype(BF16).reshape(rows, -1, HEAD_DIM)
    v_new = jnp.dot(hidden, w_v, preferred_element_type=F32).astype(BF16).reshape(rows, -1, HEAD_DIM)
    q_rot = apply_rope(rms_norm(q_raw.astype(F32), q_gain.astype(F32)), positions).astype(BF16)
    k_new = apply_rope(rms_norm(k_raw.astype(F32), k_gain.astype(F32)), positions).astype(BF16)
    return q_rot, k_new, v_new


def flip(me, rel):
    out = 0
    for bit in (1, 2, 4):
        mine = (me // bit) % 2
        out = out + bit * ((1 - mine) if rel & bit else mine)
    return out


def attn_kernel(rows, seg, width, q_in, kt, vt, kn, vn, o_out,
                qbuf, kbuf, vbuf, ostage, scores, acc, peak_ref, sum_ref, chunk_max, send, recv):
    dp = lax.axis_index("dp")
    me = lax.axis_index("cp")
    new = 8 * rows
    cols = HEADS_PER_TILE * rows
    tiles_per_slot = width // (HEADS_PER_TILE * HEAD_DIM)
    tiles = 8 * tiles_per_slot
    keys_a = 2 * seg
    keys_b = 2 * seg + new
    coef = math.log2(math.e) * HEAD_DIM ** -0.5
    neg = float("-inf")

    barrier = pltpu.get_barrier_semaphore()
    for rel in range(1, 8):
        pl.semaphore_signal(barrier, inc=1, device_id=(dp, flip(me, rel)), device_id_type=MESH)
    pl.semaphore_wait(barrier, 7)

    def qcols(who):
        return pl.ds(pl.multiple_of(who * width, width), width)

    def pieces(p):
        peer = flip(me, ORD[p])
        return {
            "q": (0, q_in.at[:, qcols(peer)], qbuf.at[p]),
            "k": (1, kt.at[peer], kbuf.at[pl.ds(p * seg, seg), :]),
            "v": (2, vt.at[peer], vbuf.at[:, pl.ds(p * seg, seg)]),
            "kn": (3, kn.at[peer], kbuf.at[pl.ds(pl.multiple_of(8 * seg + me * rows, rows), rows), :]),
            "vn": (4, vn.at[peer], vbuf.at[:, pl.ds(pl.multiple_of(8 * seg + me * rows, rows), rows)]),
            "o": (5, ostage.at[p], o_out.at[:, qcols(me)]),
        }

    def copy_of(p, what):
        kind, src, dst = pieces(p)[what]
        if p == 0:
            return pltpu.make_async_copy(src, dst, recv.at[kind, 0])
        return pltpu.make_async_remote_copy(
            src_ref=src, dst_ref=dst, send_sem=send.at[kind, p], recv_sem=recv.at[kind, p],
            device_id=(dp, flip(me, ORD[p])), device_id_type=MESH)

    def wait_in(p, what):
        c = copy_of(p, what)
        if p == 0:
            c.wait()
        else:
            c.wait_recv()

    for p in range(8):
        copy_of(p, "q").start()
        if p < 2:
            copy_of(p, "k").start()
            copy_of(p, "v").start()
    for p in range(2, 8):
        copy_of(p, "k").start()
        copy_of(p, "v").start()
    for p in range(8):
        copy_of(p, "kn").start()
        copy_of(p, "vn").start()

    def init(t, carry):
        peak_ref[t] = jnp.full((1, cols), neg, F32)
        sum_ref[t] = jnp.zeros((1, cols), F32)
        acc[t] = jnp.zeros((HEAD_DIM, cols), F32)
        return carry

    lax.fori_loop(0, tiles, init, 0)

    def q_tile(t):
        slot, part = t // tiles_per_slot, t % tiles_per_slot
        first = pl.multiple_of(part * HEADS_PER_TILE * HEAD_DIM, HEADS_PER_TILE * HEAD_DIM)
        block = qbuf[slot, :, pl.ds(first, HEADS_PER_TILE * HEAD_DIM)]
        return jnp.concatenate(
            [block[:, h * HEAD_DIM:(h + 1) * HEAD_DIM] for h in range(HEADS_PER_TILE)], axis=0)

    def step(pv=None, qk=None):
        if pv is not None:
            t, base, keys_p = pv
            old = peak_ref[t]
            top = jnp.maximum(old, jnp.max(chunk_max[...], axis=0, keepdims=True) * coef)
            fade = jnp.exp2(old - top)
            peak_ref[t] = top
        if qk is not None:
            tq, base_q, keys_q, owner = qk
            q = q_tile(tq)
        total = None
        values = None
        peaks = None
        for s in range(max(pv[2] if pv else 0, qk[2] if qk else 0) // SUB):
            lines = slice(s * SUB, (s + 1) * SUB)
            if pv is not None and s * SUB < keys_p:
                w = jnp.exp2(scores[lines, :] * coef - top)
                part = jnp.sum(w.reshape(SUB // 8, 8, cols), axis=0)
                total = part if total is None else total + part
                v_part = vbuf[:, pl.ds(pl.multiple_of(base + s * SUB, SUB), SUB)]
                o_part = jnp.dot(v_part, w.astype(BF16), preferred_element_type=F32)
                values = o_part if values is None else values + o_part
            if qk is not None and s * SUB < keys_q:
                k_part = kbuf[pl.ds(pl.multiple_of(base_q + s * SUB, SUB), SUB), :]
                sc = lax.dot_general(k_part, q, (((1,), (1,)), ((), ())), preferred_element_type=F32)
                if owner is not None and s * SUB >= keys_a:
                    key = lax.broadcasted_iota(jnp.int32, (SUB, cols), 0) + (s * SUB - keys_a)
                    row = lax.broadcasted_iota(jnp.int32, (SUB, cols), 1) % rows + owner * rows
                    sc = jnp.where(key <= row, sc, neg)
                scores[lines, :] = sc
                part = jnp.max(sc.reshape(SUB // 8, 8, cols), axis=0)
                peaks = part if peaks is None else jnp.maximum(peaks, part)
        if qk is not None:
            chunk_max[...] = peaks
        if pv is None:
            return None
        sums = sum_ref[t] * fade + jnp.sum(total, axis=0, keepdims=True)
        return sums, acc[t] * fade + values

    def keep(t, result):
        sum_ref[t], acc[t] = result

    def finish(t, result):
        sums, whole = result
        done = whole / sums
        slot, part = t // tiles_per_slot, t % tiles_per_slot
        first = pl.multiple_of(part * HEADS_PER_TILE * HEAD_DIM, HEADS_PER_TILE * HEAD_DIM)
        ostage[slot, :, pl.ds(first, HEADS_PER_TILE * HEAD_DIM)] = jnp.concatenate(
            [done[:, h * rows:(h + 1) * rows].T.astype(BF16) for h in range(HEADS_PER_TILE)], axis=1)

    for p in (0, 1):
        wait_in(p, "q") if p == 0 else None
        wait_in(p, "k")
        wait_in(p, "v")
    step(qk=(0, 0, keys_a, None))
    steps_a = 3 * tiles

    def body_a(i, carry):
        for p in range(1, 8):
            @pl.when(i + 1 == p * tiles_per_slot)
            def _():
                wait_in(p, "q")
        for v in (1, 2):
            @pl.when(i + 1 == v * tiles)
            def _():
                for p in (2 * v, 2 * v + 1):
                    wait_in(p, "k")
                    wait_in(p, "v")
        nxt = i + 1
        t = i % tiles
        keep(t, step(pv=(t, (i // tiles) * keys_a, keys_a),
                     qk=(nxt % tiles, (nxt // tiles) * keys_a, keys_a, None)))
        return carry

    lax.fori_loop(0, steps_a - 1, body_a, 0)

    for p in (6, 7):
        wait_in(p, "k")
        wait_in(p, "v")
    for p in range(8):
        wait_in(p, "kn")
        wait_in(p, "vn")

    def tile_b(i):
        return (7 - i // tiles_per_slot) * tiles_per_slot + i % tiles_per_slot

    def owner_of(i):
        slot = 7 - i // tiles_per_slot
        b0, b1, b2 = slot % 2, (slot // 2) % 2, slot // 4
        swap = b0 * b1 * (1 - b2) + (1 - b0) * (1 - b1) * b2
        r0 = (b0 + swap) % 2
        r1 = (b1 + swap) % 2
        r2 = (b2 + swap) % 2
        return (me % 2 + r0) % 2 + 2 * ((me // 2 + r1) % 2) + 4 * ((me // 4 + r2) % 2)

    last_t = tiles - 1
    base_b = 3 * keys_a
    keep(last_t, step(pv=(last_t, 2 * keys_a, keys_a), qk=(tile_b(0), base_b, keys_b, owner_of(0))))

    def body_b(i, carry):
        for p in range(7, 0, -1):
            @pl.when(i == (8 - p) * tiles_per_slot)
            def _():
                copy_of(p, "o").start()
        t = tile_b(i)
        finish(t, step(pv=(t, base_b, keys_b), qk=(tile_b(i + 1), base_b, keys_b, owner_of(i + 1))))
        return carry

    lax.fori_loop(0, tiles - 1, body_b, 0)
    t = tiles_per_slot - 1
    finish(t, step(pv=(t, base_b, keys_b)))
    copy_of(0, "o").start()
    for p in range(8):
        wait_in(p, "o")
    for p in range(1, 8):
        for what in ("q", "k", "v", "kn", "vn", "o"):
            copy_of(p, what).wait_send()


def attend(q, kt, vt, kn, vn):
    rows = q.shape[0]
    kv_heads, seg, _ = kt.shape
    width = q.shape[1] // kv_heads
    new = 8 * rows
    cols = HEADS_PER_TILE * rows
    tiles = 8 * width // (HEADS_PER_TILE * HEAD_DIM)
    keys_b = 2 * seg + new
    flops = 4 * (8 * seg + new) * 8 * rows * width
    return pl.pallas_call(
        functools.partial(attn_kernel, rows, seg, width),
        out_shape=jax.ShapeDtypeStruct(q.shape, BF16),
        in_specs=[pl.BlockSpec(memory_space=pl.ANY)] * 5,
        out_specs=pl.BlockSpec(memory_space=pl.ANY),
        scratch_shapes=[
            pltpu.VMEM((8, rows, width), BF16),
            pltpu.VMEM((8 * seg + new, HEAD_DIM), BF16),
            pltpu.VMEM((HEAD_DIM, 8 * seg + new), BF16),
            pltpu.VMEM((8, rows, width), BF16),
            pltpu.VMEM((keys_b, cols), F32),
            pltpu.VMEM((tiles, HEAD_DIM, cols), F32),
            pltpu.VMEM((tiles, 1, cols), F32),
            pltpu.VMEM((tiles, 1, cols), F32),
            pltpu.VMEM((8, cols), F32),
            pltpu.SemaphoreType.DMA((6, 8)),
            pltpu.SemaphoreType.DMA((6, 8)),
        ],
        compiler_params=pltpu.CompilerParams(
            collective_id=0, has_side_effects=True, vmem_limit_bytes=60 * 1024 * 1024),
        cost_estimate=pl.CostEstimate(flops=flops, bytes_accessed=32 * 1024 * 1024, transcendentals=flops // 512),
        name="attend",
    )(q, kt, vt, kn, vn)


def solution(mesh):
    cp_size = mesh.shape['cp']
    row_spec = P(('dp', 'cp'), None)
    cache_spec = P(('dp', 'cp'), None, None)
    whole = P()

    def device_step(x_rows, k_cache, v_cache, ln_gain, w_q, w_k, w_v, w_o, q_gain, k_gain):
        rows = x_rows.shape[0]
        prefix_len = k_cache.shape[0] * cp_size
        my_index = lax.axis_index('cp')
        row_ids = my_index * rows + jnp.arange(rows)
        x_wide = x_rows.astype(F32)
        q_rot, k_new, v_new = project_rows(x_wide, ln_gain, w_q, w_k, w_v, q_gain, k_gain, prefix_len + row_ids)
        attended = attend(
            q_rot.reshape(rows, -1),
            jnp.transpose(k_cache, (1, 0, 2)),
            jnp.transpose(v_cache, (1, 2, 0)),
            jnp.transpose(k_new, (1, 0, 2)),
            jnp.transpose(v_new, (1, 2, 0)),
        )
        out = (x_wide + jnp.dot(attended, w_o, preferred_element_type=F32)).astype(BF16)
        return out, k_new, v_new

    return jax.shard_map(device_step, mesh=mesh, in_specs=(row_spec, cache_spec, cache_spec, whole, whole, whole, whole, whole, whole, whole), out_specs=(row_spec, cache_spec, cache_spec), check_vma=False)
```

time: 1850 us -> 386 us (0.21)
  waiting for transfers between devices: 631 us -> 0 us
  matrix products: 733 us -> 109 us
  other arithmetic: 336 us -> 13.4 us
  Pallas kernels: 0 us -> 234 us
  local copies, waits for them, and re-layouts: 91.4 us -> 22.1 us
  blocking collectives: 22.9 us -> 0 us
    dot_general x36 -> x4, matrix products: 733 us -> 109 us  [the longest x1 49.9 us: project_rows(): jnp.dot(hidden, w_q, preferred_element_type=F32).astype(BF16)]
    all_to_all x1 -> x0, waiting for transfers between devices: 520 us -> none  [device_step(): lax.all_to_all(piece, 'cp', 0, 0, tiled=True)]
    reduce_sum x19 -> x0, other arithmetic: 305 us -> none  [the longest x16 264 us: partial_attend(): return (peak, jnp.sum(weights, axis=-1), weighted)]
    pallas_call x0 -> x1, Pallas kernels: none -> 234 us  [attend(): pl.pallas_call(functools.partial(attn_kernel, rows, seg, width), out_shap...]
    all_gather x3 -> x0, waiting for transfers between devices: 110 us -> none  [the longest x1 110 us: device_step(): every_q = lax.all_gather(q_grp, 'cp')]
    dynamic_slice x32 -> x0, local copies, waits for them, and re-layouts: 37.7 us -> none  [device_step(): lax.map(block_work, (every_q, every_k, every_v, jnp.arange(cp_size)))]
    all_to_all x2 -> x0, blocking collectives: 22.9 us -> none  [device_step(): lax.all_to_all(piece, 'cp', 0, 0, tiled=True)]
  transfers between devices with their start and end apart: 4 -> 0, of which waited for: 2 -> 0; matrix products, arithmetic and copies ran while one was open for 7% -> 0% of each run, Pallas kernels for 0% -> 0%
where the time goes in v1:
time: 386 us; the launch traced here: 379 us
  Pallas kernels  234 us (61%)
  matrix products  109 us (28%)
  local copies, waits for them, and re-layouts  22.1 us (6%)
  other arithmetic  13.4 us (3%)
    pallas_call x1, Pallas kernels, attend(): pl.pallas_call(functools.partial(attn_kernel, rows, seg, width), out_shap...  234 us
    dot_general x1, matrix products, project_rows(): jnp.dot(hidden, w_q, preferred_element_type=F32).astype(BF16)  49.9 us
    dot_general x1, matrix products, device_step(): jnp.dot(attended, w_o, preferred_element_type=F32)  49.8 us
    unnamed x28, local copies, waits for them, and re-layouts  20.8 us

profile of v1, /device:TPU:0, one launch (start us, length us, event | category | flops | bytes accessed | tf_op | source)
XLA Modules:
  0.0 379.4 jit_solution(12689785125565633303)
XLA Ops:
  0.6 0.7 convert_element_type.54
  1.3 1.8 fusion.2
  3.1 0.0 copy-start.6
  3.2 6.9 %fusion.6 = f32[128,1024]{1,0:T(8,128)S(1)} fusion(bf16[6144,1024]{1,0:T(8,128)(2,1)} %param.15, bf16[128,6144]{1,0:T(8,128)(2,1)} %param.10, f32[6144]{0:T(1024)S(1)} %convert_element_type.54, f32[128]{0:T(128)S(1)} %add_rsqrt_fusion.2), kind=kOutput, calls=%fused_computation.19 | convolution fusion | flops 1614020608 | bytes 14705152 | tf_op jit(solution)/shard_map/dot_general | solution.py:43
  10.1 0.0 copy-start
  10.1 0.2 copy.20
  10.3 0.2 copy.21
  10.6 0.0 copy-done.6
  10.6 0.2 multiply_multiply_fusion.1
  10.8 0.3 multiply_cosine_fusion
  11.1 0.3 subtract_convert_fusion.1
  11.4 0.0 copy-start.1
  11.4 0.0 copy-start.3
  11.4 0.7 copy-done.1
  12.1 0.1 copy-done.3
  12.2 0.8 fusion.15.kn
  13.0 0.0 copy-done
  13.0 49.9 %fusion.5 = f32[16,8,96,128]{3,1,2,0:T(8,128)} fusion(bf16[6144,12288]{1,0:T(8,128)(2,1)} %param.14, bf16[128,6144]{1,0:T(8,128)(2,1)S(1)} %copy-done, f32[6144]{0:T(1024)S(1)} %convert_element_type.54, f32[128]{0:T(128)S(1)} %add_rsqrt_fusion.2), kind=kOutput, calls=%fused_computation.16 | convolution fusion | flops 19333644288 | bytes 158884352 | tf_op jit(solution)/shard_map/dot_general | solution.py:42
  63.0 3.9 %copy.25 = f32[16,8,96,128]{3,2,1,0:T(8,128)S(1)} copy(f32[16,8,96,128]{3,1,2,0:T(8,128)} %fusion.5) | data formatting | bytes 12582912
  66.8 0.0 copy-start.7
  66.8 2.2 multiply_reduce_fusion
  69.1 0.0 copy-done.7
  69.1 2.4 multiply_multiply_fusion
  71.5 0.0 slice-start
  71.5 0.0 slice-start.1
  71.5 2.7 subtract_convert_fusion
  74.2 0.0 slice-start.2
  74.2 1.7 pad_maximum_fusion
  76.0 3.0 copy.30
  79.0 0.0 slice-done
  79.0 0.0 slice-done.1
  79.0 0.0 slice-done.2
  79.0 2.0 convolution_convert_fusion.1
  81.0 0.8 copy.22
  81.8 6.7 %copy.19 = bf16[2048,8,128]{0,2,1:T(8,128)(2,1)} copy(bf16[2048,8,128]{2,1,0:T(8,128)(2,1)} %param.12) | data formatting | bytes 8388608 | tf_op args[2]
  88.5 4.7 %copy.29 = bf16[2048,8,128]{2,0,1:T(8,128)(2,1)} copy(bf16[2048,8,128]{2,1,0:T(8,128)(2,1)} %param.11) | data formatting | bytes 8388608 | tf_op args[1]
  93.2 234.4 %attend.1 = bf16[128,12288]{1,0:T(8,128)(2,1)} custom-call(bf16[128,12288]{1,0:T(8,128)(2,1)} %bitcast.31, bf16[8,2048,128]{2,1,0:T(8,128)(2,1)} %bitcast.30, bf16[8,128,2048]{2,1,0:T(8,128)(2,1)} %bitcast.29, bf16[8,128,128]{2,1,0:T(8,128)(2,1)} %fusion.15.kn, bf16[8,128,128]{2,1,0:T(8,128)(2,1)} %bitcast.32), custom_call_target="tpu_custom_call" | custom-call | flops 109521666048 | bytes 33554432 | tf_op jit(solution)/shard_map/attend/pallas_call | solution.py:260
  327.6 0.0 copy-start.2
  327.6 0.0 copy-start.4
  327.6 0.0 copy-start.5
  327.6 49.8 %fusion.1 = bf16[128,6144]{1,0:T(8,128)(2,1)} fusion(bf16[128,12288]{1,0:T(8,128)(2,1)} %attend.1, bf16[12288,6144]{1,0:T(8,128)(2,1)} %param.17, bf16[128,6144]{1,0:T(8,128)(2,1)S(1)} %copy-done), kind=kOutput, calls=%fused_computation.3 | convolution fusion | flops 19329712128 | bytes 157286400 | tf_op jit(solution)/shard_map/dot_general | solution.py:305
  377.4 0.0 copy-done.2
  377.4 0.0 copy-done.4
  377.4 0.1 pad_maximum_fusion.1
  377.6 0.9 copy.23
  378.5 0.0 copy-done.5
  378.5 0.9 copy.24
  (9 shorter events, 0.1 us)
Async XLA Ops:
  3.1 7.4 %copy-start.6 = (bf16[128]{0:T(256)(128)(2,1)S(1)}, bf16[128]{0:T(256)(128)(2,1)}, u32[]{:S(2)}) copy-start(bf16[128]{0:T(256)(128)(2,1)} %param.19) | copy-start | bytes 772
  10.1 3.0 copy-start
  11.4 0.7 copy-start.1
  11.4 0.8 copy-start.3
  66.8 2.3 copy-start.7
  71.5 7.5 %slice-start = ((s8[12582912]{0:T(1024)(128)(4,1)}), s8[4194304]{0:T(1024)(128)(4,1)S(1)}, s32[]{:S(2)}) async-start(s8[12582912]{0:T(1024)(128)(4,1)} %bitcast.34), calls=%async_computation | async-start | bytes 8388608
  71.5 7.5 %slice-start.1 = ((s8[12582912]{0:T(1024)(128)(4,1)}), s8[4194304]{0:T(1024)(128)(4,1)S(1)}, s32[]{:S(2)}) async-start(s8[12582912]{0:T(1024)(128)(4,1)} %bitcast.34), calls=%async_computation.1 | async-start | bytes 8388608
  74.2 4.8 %slice-start.2 = ((s8[12582912]{0:T(1024)(128)(4,1)}), s8[4194304]{0:T(1024)(128)(4,1)S(1)}, s32[]{:S(2)}) async-start(s8[12582912]{0:T(1024)(128)(4,1)} %bitcast.34), calls=%async_computation.2 | async-start | bytes 8388608
  327.6 49.9 %copy-start.2 = (bf16[128,8,64]{2,0,1:T(8,128)(2,1)S(1)}, bf16[128,8,64]{2,0,1:T(8,128)(2,1)}, u32[]{:S(2)}) copy-start(bf16[128,8,64]{2,0,1:T(8,128)(2,1)} %copy-done.1) | copy-start | bytes 393220
  327.6 49.9 %copy-start.4 = (bf16[128,8,64]{2,0,1:T(8,128)(2,1)S(1)}, bf16[128,8,64]{2,0,1:T(8,128)(2,1)}, u32[]{:S(2)}) copy-start(bf16[128,8,64]{2,0,1:T(8,128)(2,1)} %copy-done.3) | copy-start | bytes 393220
  327.6 50.9 %copy-start.5 = (bf16[128,1024]{0,1:T(8,128)(2,1)S(1)}, bf16[128,1024]{0,1:T(8,128)(2,1)}, u32[]{:S(2)}) copy-start(bf16[128,1024]{0,1:T(8,128)(2,1)} %copy.22) | copy-start | bytes 786436

commit v2 on v0

v2 whole, which is shorter than its diff:
```python
import functools
import math

import jax
import jax.numpy as jnp
from jax import lax
from jax.experimental import pallas as pl
from jax.experimental.pallas import tpu as pltpu
from jax.sharding import PartitionSpec as P

HEAD_DIM = 128
ROPE_THETA = 1.0e6
NORM_EPS = 1.0e-6
MESH = pl.DeviceIdType.MESH
F32 = jnp.float32
BF16 = jnp.bfloat16

ORD = (0, 1, 2, 4, 3, 5, 6, 7)
SUB = 256
TILE = 512
HEADS = TILE // HEAD_DIM
WBUFS = 3


def flip(me, rel):
    out = 0
    for bit in (1, 2, 4):
        mine = (me // bit) % 2
        out = out + bit * ((1 - mine) if rel & bit else mine)
    return out


def flip_chip(chip, rel):
    return (chip % 2 + rel % 2) % 2 + 2 * ((chip // 2 + rel // 2) % 2)


def block_kernel(rows, seg, width,
                 x_in, kt, vt, ln_in, gain_in, cos_in, sin_in, wq_in, wk_in, wv_in, wo_in,
                 out, k_out, v_out,
                 xbuf, hbuf, wbuf, raw, stage, vstage, qbuf, kbuf, vbuf, scores, acc, peak_ref, sum_ref, chunk_max, outst,
                 wsem, xsem, qsend, qrecv, kvsend, kvrecv, nsend, nrecv, osend, orecv, ksend, krecv, psend, precv, outsem,
                 free_sem):
    dp = lax.axis_index("dp")
    me = lax.axis_index("cp")
    chip, core = me // 2, me % 2
    hid = wbuf.shape[1]
    pair = 2 * rows
    new = 8 * rows
    parts = width // TILE
    per_chip = 2 * parts
    tiles = 4 * per_chip
    keys_a = 2 * seg
    keys_b = 2 * seg + new
    coef = math.log2(math.e) * HEAD_DIM ** -0.5
    neg = float("-inf")
    q_tiles = 4 * parts
    p1_tiles = q_tiles + 2
    out_tiles = hid // TILE
    chunk = hid // 4

    def device(index):
        return (dp, index)

    partner = flip(me, 1)

    barrier = pltpu.get_barrier_semaphore()
    for rel in range(1, 8):
        pl.semaphore_signal(barrier, inc=1, device_id=device(flip(me, rel)), device_id_type=MESH)
    pl.semaphore_wait(barrier, 7)

    def remote(src, dst, send, recv, index):
        return pltpu.make_async_remote_copy(
            src_ref=src, dst_ref=dst, send_sem=send, recv_sem=recv, device_id=device(index), device_id_type=MESH)

    my_rows = pl.ds(pl.multiple_of(core * rows, rows), rows)
    other_rows = pl.ds(pl.multiple_of((1 - core) * rows, rows), rows)

    def tile_of(ref, slot, a):
        return ref.at[slot, pl.ds(a * chunk, chunk), :]

    def fetch_kv(ref, n):
        slot = n % WBUFS
        for a in range(4):
            first = pl.multiple_of((2 * a + core) * HEAD_DIM, HEAD_DIM)
            pltpu.make_async_copy(ref.at[:, pl.ds(first, HEAD_DIM)],
                                  wbuf.at[slot, :, pl.ds(a * HEAD_DIM, HEAD_DIM)], wsem.at[slot, a]).start()

    def fetch_q(n):
        slot = n % WBUFS
        g, part = (n - 1) // parts, (n - 1) % parts
        head = 2 * flip_chip(chip, (g + 1) % 4) + core
        first = pl.multiple_of(head * width + part * TILE, TILE)
        for a in range(4):
            pltpu.make_async_copy(wq_in.at[pl.ds(a * chunk, chunk), pl.ds(first, TILE)],
                                  tile_of(wbuf, slot, a), wsem.at[slot, a]).start()

    def fetch_o(m):
        slot = (p1_tiles + m) % WBUFS
        first = pl.multiple_of(m * TILE, TILE)
        for a in range(4):
            top = pl.multiple_of((2 * a + core) * width, width)
            pltpu.make_async_copy(wo_in.at[pl.ds(top, width), pl.ds(first, TILE)],
                                  tile_of(wbuf, slot, a), wsem.at[slot, a]).start()

    def wait_tile(n):
        slot = n % WBUFS
        for a in range(4):
            pltpu.make_async_copy(tile_of(wbuf, slot, a), tile_of(wbuf, slot, a), wsem.at[slot, a]).wait()

    x_local = pltpu.make_async_copy(x_in, xbuf.at[my_rows, :], xsem.at[0])
    x_remote = remote(x_in, xbuf.at[my_rows, :], xsem.at[1], xsem.at[2], partner)
    x_local.start()
    x_remote.start()
    fetch_kv(wk_in, 0)
    fetch_q(1)
    fetch_q(2)

    def kv_copy(p, kind):
        peer = flip(me, ORD[p])
        if kind == 0:
            src, dst = kt.at[peer], kbuf.at[pl.ds(p * seg, seg), :]
        else:
            src, dst = vt.at[peer], vbuf.at[:, pl.ds(p * seg, seg)]
        if p == 0:
            return pltpu.make_async_copy(src, dst, kvrecv.at[kind, 0])
        return remote(src, dst, kvsend.at[kind, p], kvrecv.at[kind, p], peer)

    def kv_wait(p):
        for kind in range(2):
            if p == 0:
                kv_copy(p, kind).wait()
            else:
                kv_copy(p, kind).wait_recv()

    for p in range(2):
        for kind in range(2):
            kv_copy(p, kind).start()

    def normalise(first_row):
        def some(i, carry):
            at = pl.multiple_of(first_row + i * 16, 16)
            wide = xbuf[pl.ds(at, 16), :].astype(F32)
            mean_sq = jnp.sum(wide * wide, axis=-1, keepdims=True) * (1.0 / hid)
            hbuf[pl.ds(at, 16), :] = (wide * lax.rsqrt(mean_sq + NORM_EPS) * ln_in[...]).astype(BF16)
            return carry
        lax.fori_loop(0, rows // 16, some, 0)

    x_local.wait()
    normalise(core * rows)
    x_remote.wait_recv()
    normalise((1 - core) * rows)

    def multiply(n):
        slot = n % WBUFS
        return jnp.dot(hbuf[...], wbuf[slot], preferred_element_type=F32)

    def rotate(e):
        group, part = (e + parts - 1) // parts, (e + parts - 1) % parts
        gain = gain_in[jnp.minimum(e, 1)]
        cos_tab, sin_tab = cos_in[...], sin_in[...]
        done = []
        for h in range(HEADS):
            vals = raw[:, h * HEAD_DIM:(h + 1) * HEAD_DIM].astype(F32)
            mean_sq = jnp.sum(vals * vals, axis=-1, keepdims=True) * (1.0 / HEAD_DIM)
            vals = vals * lax.rsqrt(mean_sq + NORM_EPS) * gain
            done.append((vals * cos_tab + pltpu.roll(vals, HEAD_DIM // 2, 1) * sin_tab).astype(BF16))
        done = jnp.concatenate(done, axis=1)
        where = pl.ds(pl.multiple_of(part * TILE, TILE), TILE)
        stage[group, :, where] = done
        qbuf[0, :, where] = done

    def q_copy(rel, part):
        cols = pl.ds(pl.multiple_of(part * TILE, TILE), TILE)
        return remote(stage.at[rel, :, cols], qbuf.at[rel, :, cols], qsend.at[rel, part], qrecv.at[rel, part],
                      2 * flip_chip(chip, rel) + core)

    def new_copy(rel, kind):
        other = flip_chip(chip, rel)
        here = pl.ds(pl.multiple_of(8 * seg + chip * pair, pair), pair)
        if kind == 0:
            first = pl.multiple_of((parts - 1) * TILE + other * HEAD_DIM, HEAD_DIM)
            src, dst = stage.at[0, :, pl.ds(first, HEAD_DIM)], kbuf.at[here, :]
        else:
            src, dst = vstage.at[other], vbuf.at[:, here]
        return remote(src, dst, nsend.at[kind, rel], nrecv.at[kind, rel], 2 * other + core)

    k_cols = pl.ds((parts - 1) * TILE, TILE)
    new_outs = (
        (pltpu.make_async_copy(stage.at[0, my_rows, k_cols], k_out.at[core], krecv.at[0]),
         remote(stage.at[0, other_rows, k_cols], k_out.at[core], ksend.at[0], krecv.at[1], partner)),
        (pltpu.make_async_copy(raw.at[my_rows, :], v_out.at[core], krecv.at[2]),
         remote(raw.at[other_rows, :], v_out.at[core], ksend.at[1], krecv.at[3], partner)),
    )

    wait_tile(0)
    raw[...] = multiply(0).astype(BF16)
    fetch_q(3)

    def project(n, carry):
        @pl.when(n == 2)
        def _():
            for rel in range(1, 4):
                new_copy(rel, 0).start()
            for c in new_outs[0]:
                c.start()

        @pl.when((n >= 3) & (n < 3 + 3 * parts))
        def _():
            e = n - 2
            q_copy((e + parts - 1) // parts, (e + parts - 1) % parts).start()

        @pl.when(n == 3 + 3 * parts)
        def _():
            for p in range(2, 8):
                for kind in range(2):
                    kv_copy(p, kind).start()

        wait_tile(n)
        rotate(n - 1)
        raw[...] = multiply(n).astype(BF16)

        @pl.when(n + WBUFS <= q_tiles)
        def _():
            fetch_q(n + WBUFS)

        @pl.when(n + WBUFS == q_tiles + 1)
        def _():
            fetch_kv(wv_in, q_tiles + 1)

        @pl.when(n + WBUFS >= p1_tiles)
        def _():
            fetch_o(n + WBUFS - p1_tiles)

        return carry

    lax.fori_loop(1, p1_tiles, project, 0)

    here = pl.ds(pl.multiple_of(8 * seg + chip * pair, pair), pair)
    for a in range(4):
        vstage[a] = raw[:, a * HEAD_DIM:(a + 1) * HEAD_DIM].astype(F32).T.astype(BF16)
    kbuf[here, :] = stage[0, :, pl.ds(pl.multiple_of((parts - 1) * TILE + chip * HEAD_DIM, HEAD_DIM), HEAD_DIM)]
    vbuf[:, here] = vstage[chip]

    def init(t, carry):
        peak_ref[t] = jnp.full((1, TILE), neg, F32)
        sum_ref[t] = jnp.zeros((1, TILE), F32)
        acc[t] = jnp.zeros((HEAD_DIM, TILE), F32)
        return carry

    lax.fori_loop(0, tiles, init, 0)
    for rel in range(1, 4):
        new_copy(rel, 1).start()
    for c in new_outs[1]:
        c.start()

    def place(t):
        rel, rest = t // per_chip, t % per_chip
        return rel, pl.ds(pl.multiple_of((rest % 2) * rows, rows), rows), rest // 2

    def q_tile(t):
        rel, some_rows, part = place(t)
        block = qbuf[rel, some_rows, pl.ds(pl.multiple_of(part * TILE, TILE), TILE)]
        return jnp.concatenate([block[:, h * HEAD_DIM:(h + 1) * HEAD_DIM] for h in range(HEADS)], axis=0)

    def step(pv=None, qk=None):
        if pv is not None:
            t, base, keys_p = pv
            old = peak_ref[t]
            top = jnp.maximum(old, jnp.max(chunk_max[...], axis=0, keepdims=True) * coef)
            fade = jnp.exp2(old - top)
            peak_ref[t] = top
        if qk is not None:
            tq, base_q, keys_q, has_new = qk
            q = q_tile(tq)
            first_row = flip_chip(chip, tq // per_chip) * pair + (tq % 2) * rows
        total = None
        values = None
        peaks = None
        for s in range(max(pv[2] if pv else 0, qk[2] if qk else 0) // SUB):
            lines = slice(s * SUB, (s + 1) * SUB)
            if pv is not None and s * SUB < keys_p:
                w = jnp.exp2(scores[lines, :] * coef - top)
                part = jnp.sum(w.reshape(SUB // 8, 8, TILE), axis=0)
                total = part if total is None else total + part
                v_part = vbuf[:, pl.ds(pl.multiple_of(base + s * SUB, SUB), SUB)]
                o_part = jnp.dot(v_part, w.astype(BF16), preferred_element_type=F32)
                values = o_part if values is None else values + o_part
            if qk is not None and s * SUB < keys_q:
                k_part = kbuf[pl.ds(pl.multiple_of(base_q + s * SUB, SUB), SUB), :]
                sc = lax.dot_general(k_part, q, (((1,), (1,)), ((), ())), preferred_element_type=F32)
                if has_new and s * SUB >= keys_a:
                    key = lax.broadcasted_iota(jnp.int32, (SUB, TILE), 0) + (s * SUB - keys_a)
                    row = lax.broadcasted_iota(jnp.int32, (SUB, TILE), 1) % rows + first_row
                    sc = jnp.where(key <= row, sc, neg)
                scores[lines, :] = sc
                part = jnp.max(sc.reshape(SUB // 8, 8, TILE), axis=0)
                peaks = part if peaks is None else jnp.maximum(peaks, part)
        if qk is not None:
            chunk_max[...] = peaks
        if pv is None:
            return None
        sums = sum_ref[t] * fade + jnp.sum(total, axis=0, keepdims=True)
        return sums, acc[t] * fade + values

    def keep(t, result):
        sum_ref[t], acc[t] = result

    def finish(t, result):
        sums, whole = result
        done = whole / sums
        rel, some_rows, part = place(t)
        done = jnp.concatenate([done[:, h * rows:(h + 1) * rows].T.astype(BF16) for h in range(HEADS)], axis=1)
        stage[rel, some_rows, pl.ds(pl.multiple_of(part * TILE, TILE), TILE)] = done
        hbuf[some_rows, pl.ds(pl.multiple_of(chip * width + part * TILE, TILE), TILE)] = done

    kv_wait(0)
    kv_wait(1)
    step(qk=(0, 0, keys_a, False))
    steps_a = 3 * tiles

    def body_a(i, carry):
        nxt = i + 1

        @pl.when((nxt >= per_chip) & (nxt < tiles) & (nxt % 2 == 0))
        def _():
            q_copy(nxt // per_chip, (nxt % per_chip) // 2).wait_recv()

        for v in (1, 2):
            @pl.when(nxt == v * tiles)
            def _():
                kv_wait(2 * v)
                kv_wait(2 * v + 1)
        t = i % tiles
        keep(t, step(pv=(t, (i // tiles) * keys_a, keys_a),
                     qk=(nxt % tiles, (nxt // tiles) * keys_a, keys_a, False)))
        return carry

    lax.fori_loop(0, steps_a - 1, body_a, 0)

    kv_wait(6)
    kv_wait(7)
    for rel in range(1, 4):
        new_copy(rel, 0).wait_recv()
        new_copy(rel, 1).wait_recv()
        new_copy(rel, 0).wait_send()
        for part in range(parts):
            q_copy(rel, part).wait_send()
    new_outs[0][0].wait()
    new_outs[0][1].wait_send()

    def tile_b(i):
        return (3 - i // per_chip) * per_chip + i % per_chip

    def o_copy(rel, part):
        cols = pl.ds(pl.multiple_of(part * TILE, TILE), TILE)
        there = pl.ds(pl.multiple_of(chip * width + part * TILE, TILE), TILE)
        return remote(stage.at[rel, :, cols], hbuf.at[:, there], osend.at[rel, part], orecv.at[rel, part],
                      2 * flip_chip(chip, rel) + core)

    def o_arrival(rel, part):
        there = pl.ds(pl.multiple_of(flip_chip(chip, rel) * width + part * TILE, TILE), TILE)
        return remote(hbuf.at[:, there], hbuf.at[:, there], osend.at[rel, part], orecv.at[rel, part],
                      2 * flip_chip(chip, rel) + core)

    last_t = tiles - 1
    base_b = 3 * keys_a
    keep(last_t, step(pv=(last_t, 2 * keys_a, keys_a), qk=(tile_b(0), base_b, keys_b, True)))

    def body_b(i, carry):
        @pl.when((i >= 2) & (i % 2 == 0) & (i <= 3 * per_chip))
        def _():
            done = i - 2
            o_copy(3 - done // per_chip, (done % per_chip) // 2).start()

        t = tile_b(i)
        finish(t, step(pv=(t, base_b, keys_b), qk=(tile_b(i + 1), base_b, keys_b, True)))
        return carry

    lax.fori_loop(0, tiles - 1, body_b, 0)
    finish(per_chip - 1, step(pv=(per_chip - 1, base_b, keys_b)))

    pl.semaphore_signal(free_sem, inc=1, device_id=device(partner), device_id_type=MESH)
    for rel in range(1, 4):
        for part in range(parts):
            o_arrival(rel, part).wait_recv()
    pl.semaphore_wait(free_sem, 1)

    sent, got, own = 0, out_tiles * rows, 2 * out_tiles * rows

    def lines(first, m):
        return pl.ds(pl.multiple_of(first + m * rows, rows), rows)

    def p_copy(m):
        return remote(scores.at[lines(sent, m), :], scores.at[lines(got, m), :], psend.at[m], precv.at[m], partner)

    def out_copy(m):
        cols = pl.ds(pl.multiple_of(m * TILE, TILE), TILE)
        return pltpu.make_async_copy(outst.at[:, cols], out.at[:, cols], outsem.at[m])

    def combine(m):
        p_copy(m).wait_recv()
        cols = pl.ds(pl.multiple_of(m * TILE, TILE), TILE)
        both = scores[lines(own, m), :] + scores[lines(got, m), :]
        outst[:, cols] = (xbuf[my_rows, cols].astype(F32) + both).astype(BF16)
        out_copy(m).start()

    def output(m, carry):
        @pl.when(m >= 1)
        def _():
            p_copy(m - 1).start()

        @pl.when(m >= 2)
        def _():
            combine(m - 2)

        wait_tile(p1_tiles + m)
        both = multiply(p1_tiles + m)
        scores[lines(own, m), :] = jnp.where(core == 0, both[:rows], both[rows:])
        scores[lines(sent, m), :] = jnp.where(core == 0, both[rows:], both[:rows])

        @pl.when(m + WBUFS < out_tiles)
        def _():
            fetch_o(m + WBUFS)

        return carry

    lax.fori_loop(0, out_tiles, output, 0)
    p_copy(out_tiles - 1).start()
    combine(out_tiles - 2)
    combine(out_tiles - 1)

    def drain(m, carry):
        p_copy(m).wait_send()
        out_copy(m).wait()
        return carry

    lax.fori_loop(0, out_tiles, drain, 0)
    x_remote.wait_send()
    for p in range(1, 8):
        for kind in range(2):
            kv_copy(p, kind).wait_send()
    for rel in range(1, 4):
        new_copy(rel, 1).wait_send()
        for part in range(parts):
            o_copy(rel, part).wait_send()
    new_outs[0][1].wait_recv()
    new_outs[1][0].wait()
    new_outs[1][1].wait()


def block(x, kt, vt, ln, gains, cos_tab, sin_tab, w_q, w_k, w_v, w_o):
    rows, hid = x.shape
    _, seg, _ = kt.shape
    width = w_q.shape[1] // 8
    pair, new = 2 * rows, 8 * rows
    parts = width // TILE
    tiles = 8 * parts
    out_tiles = hid // TILE
    keys_b = 2 * seg + new
    flops = 4 * (8 * seg + new) * 8 * rows * width + 8 * rows * hid * width * 2
    hbm = pl.BlockSpec(memory_space=pl.ANY)
    vmem = pl.BlockSpec(memory_space=pltpu.VMEM)
    dma = pltpu.SemaphoreType.DMA
    return pl.pallas_call(
        functools.partial(block_kernel, rows, seg, width),
        out_shape=(
            jax.ShapeDtypeStruct((rows, hid), BF16),
            jax.ShapeDtypeStruct((2, rows, TILE), BF16),
            jax.ShapeDtypeStruct((2, rows, TILE), BF16),
        ),
        in_specs=[hbm, hbm, hbm, vmem, vmem, vmem, vmem, hbm, hbm, hbm, hbm],
        out_specs=(hbm, hbm, hbm),
        scratch_shapes=[
            pltpu.VMEM((pair, hid), BF16),
            pltpu.VMEM((pair, hid), BF16),
            pltpu.VMEM((WBUFS, hid, TILE), BF16),
            pltpu.VMEM((pair, TILE), BF16),
            pltpu.VMEM((5, pair, width), BF16),
            pltpu.VMEM((4, HEAD_DIM, pair), BF16),
            pltpu.VMEM((4, pair, width), BF16),
            pltpu.VMEM((8 * seg + new, HEAD_DIM), BF16),
            pltpu.VMEM((HEAD_DIM, 8 * seg + new), BF16),
            pltpu.VMEM((max(keys_b, 3 * out_tiles * rows), TILE), F32),
            pltpu.VMEM((tiles, HEAD_DIM, TILE), F32),
            pltpu.VMEM((tiles, 1, TILE), F32),
            pltpu.VMEM((tiles, 1, TILE), F32),
            pltpu.VMEM((8, TILE), F32),
            pltpu.VMEM((rows, hid), BF16),
            dma((WBUFS, 4)),
            dma((3,)),
            dma((4, parts)), dma((4, parts)),
            dma((2, 8)), dma((2, 8)),
            dma((2, 4)), dma((2, 4)),
            dma((4, parts)), dma((4, parts)),
            dma((2,)), dma((4,)),
            dma((out_tiles,)), dma((out_tiles,)),
            dma((out_tiles,)),
            pltpu.SemaphoreType.REGULAR,
        ],
        compiler_params=pltpu.CompilerParams(
            collective_id=0, has_side_effects=True, vmem_limit_bytes=67043328),
        cost_estimate=pl.CostEstimate(flops=flops, bytes_accessed=200 * 1024 * 1024, transcendentals=flops // 512),
        name="block",
    )(x, kt, vt, ln, gains, cos_tab, sin_tab, w_q, w_k, w_v, w_o)


def solution(mesh):
    cp_size = mesh.shape['cp']
    row_spec = P(('dp', 'cp'), None)
    cache_spec = P(('dp', 'cp'), None, None)
    whole = P()

    def device_step(x_rows, k_cache, v_cache, ln_gain, w_q, w_k, w_v, w_o, q_gain, k_gain):
        rows = x_rows.shape[0]
        prefix_len = k_cache.shape[0] * cp_size
        chip = lax.axis_index('cp') // 2
        positions = (prefix_len + chip * 2 * rows + jnp.arange(2 * rows)).astype(F32)
        half = HEAD_DIM // 2
        inv_freq = ROPE_THETA ** (-jnp.arange(half, dtype=F32) * (2.0 / HEAD_DIM))
        angles = positions[:, None] * inv_freq[None, :]
        cos_half, sin_half = jnp.cos(angles), jnp.sin(angles)
        cos_tab = jnp.concatenate([cos_half, cos_half], axis=1)
        sin_tab = jnp.concatenate([-sin_half, sin_half], axis=1)
        gains = jnp.stack([k_gain, q_gain]).astype(F32)[:, None, :]
        out, k_pairs, v_pairs = block(
            x_rows,
            jnp.transpose(k_cache, (1, 0, 2)),
            jnp.transpose(v_cache, (1, 2, 0)),
            ln_gain.astype(F32)[None, :], gains, cos_tab, sin_tab, w_q, w_k, w_v, w_o)

        def heads(pairs):
            return jnp.transpose(pairs.reshape(2, rows, 4, HEAD_DIM), (1, 2, 0, 3)).reshape(rows, 8, HEAD_DIM)

        return out, heads(k_pairs), heads(v_pairs)

    return jax.shard_map(device_step, mesh=mesh, in_specs=(row_spec, cache_spec, cache_spec, whole, whole, whole, whole, whole, whole, whole), out_specs=(row_spec, cache_spec, cache_spec), check_vma=False)
```

time: 1850 us -> 307 us (0.17)
  matrix products: 733 us -> 0 us
  waiting for transfers between devices: 631 us -> 0 us
  other arithmetic: 336 us -> 3.96 us
  Pallas kernels: 0 us -> 284 us
  local copies, waits for them, and re-layouts: 91.4 us -> 18.3 us
  blocking collectives: 22.9 us -> 0 us
    dot_general x36 -> x0, matrix products: 733 us -> none  [the longest x16 334 us: partial_attend(): jnp.einsum('krgs,skd->krgd', weights.astype(jnp.bfloat16), vals, preferre...]
    all_to_all x1 -> x0, waiting for transfers between devices: 520 us -> none  [device_step(): lax.all_to_all(piece, 'cp', 0, 0, tiled=True)]
    reduce_sum x22 -> x0, other arithmetic: 312 us -> none  [the longest x16 264 us: partial_attend(): return (peak, jnp.sum(weights, axis=-1), weighted)]
    pallas_call x0 -> x1, Pallas kernels: none -> 284 us  [block(): pl.pallas_call(functools.partial(block_kernel, rows, seg, width), out_sha...]
    all_gather x3 -> x0, waiting for transfers between devices: 110 us -> none  [the longest x1 110 us: device_step(): every_q = lax.all_gather(q_grp, 'cp')]
    dynamic_slice x32 -> x0, local copies, waits for them, and re-layouts: 37.7 us -> none  [device_step(): lax.map(block_work, (every_q, every_k, every_v, jnp.arange(cp_size)))]
    all_to_all x2 -> x0, blocking collectives: 22.9 us -> none  [device_step(): lax.all_to_all(piece, 'cp', 0, 0, tiled=True)]
  transfers between devices with their start and end apart: 4 -> 0, of which waited for: 2 -> 0; matrix products, arithmetic and copies ran while one was open for 7% -> 0% of each run, Pallas kernels for 0% -> 0%
where the time goes in v2:
time: 307 us
  Pallas kernels  284 us (93%)
  local copies, waits for them, and re-layouts  18.3 us (6%)
  other arithmetic  3.96 us (1%)
    pallas_call x1, Pallas kernels, block(): pl.pallas_call(functools.partial(block_kernel, rows, seg, width), out_sha...  284 us
    unnamed x3, local copies, waits for them, and re-layouts  14 us

profile of v2, /device:TPU:0, one launch (start us, length us, event | category | flops | bytes accessed | tf_op | source)
XLA Modules:
  0.0 307.0 jit_solution(3266313798146792059)
XLA Ops:
  0.7 1.3 maximum_convert_fusion.gain_in
  1.9 1.3 broadcast_in_dim.10
  3.2 0.5 fusion
  3.8 0.8 pad_maximum_fusion
  4.6 4.7 %copy.18 = bf16[2048,8,128]{2,0,1:T(8,128)(2,1)} copy(bf16[2048,8,128]{2,1,0:T(8,128)(2,1)} %param.11) | data formatting | bytes 8388608 | tf_op args[1]
  9.3 6.7 %copy.14 = bf16[2048,8,128]{0,2,1:T(8,128)(2,1)} copy(bf16[2048,8,128]{2,1,0:T(8,128)(2,1)} %param.12) | data formatting | bytes 8388608 | tf_op args[2]
  16.0 284.1 %block.1 = (bf16[128,6144]{1,0:T(8,128)(2,1)}, bf16[2,128,512]{2,1,0:T(8,128)(2,1)}, bf16[2,128,512]{2,1,0:T(8,128)(2,1)}) custom-call(bf16[128,6144]{1,0:T(8,128)(2,1)} %x_in.1, bf16[8,2048,128]{2,1,0:T(8,128)(2,1)} %bitcast.11, bf16[8,128,2048]{2,1,0:T(8,128)(2,1)} %bitcast.12, f32[1,6144]{1,0:T(1,128)} %bitcast.17, ...), custom_call_target="tpu_custom_call" | custom-call | flops 128849018880 | bytes 209715200 | tf_op jit(solution)/shard_map/block/pallas_call | solution.py:464
  300.0 1.0 reshape.60
  301.1 1.1 copy.15
  302.2 1.0 reshape.62
  303.2 1.1 copy.16
  304.3 2.7 copy.20
  (2 shorter events, 0.0 us)

commit v3 on v2

v3 whole, which is shorter than its diff:
```python
import functools
import math

import jax
import jax.numpy as jnp
from jax import lax
from jax.experimental import pallas as pl
from jax.experimental.pallas import tpu as pltpu
from jax.sharding import PartitionSpec as P

HEAD_DIM = 128
ROPE_THETA = 1.0e6
NORM_EPS = 1.0e-6
MESH = pl.DeviceIdType.MESH
F32 = jnp.float32
BF16 = jnp.bfloat16

ORD = (0, 1, 2, 4, 3, 5, 6, 7)
SUB = 256
TILE = 512
HEADS = TILE // HEAD_DIM
WBUFS = 3


def div(a, b):
    return a // b if isinstance(a, int) else lax.div(a, jnp.int32(b))


def rem(a, b):
    return a % b if isinstance(a, int) else lax.rem(a, jnp.int32(b))


def flip(me, rel):
    out = 0
    for bit in (1, 2, 4):
        mine = rem(div(me, bit), 2)
        out = out + bit * ((1 - mine) if rel & bit else mine)
    return out


def flip_chip(chip, rel):
    return rem(rem(chip, 2) + rem(rel, 2), 2) + 2 * rem(div(chip, 2) + div(rel, 2), 2)


def block_kernel(rows, seg, width,
                 x_in, k_in, v_in, ln_in, gain_in, cos_in, sin_in, wq_in, wk_in, wv_in, wo_in,
                 out, k_out, v_out, kt, vt,
                 xres, hbuf, wbuf, raw, stage, vstage, qbuf, kbuf, vbuf, scores, acc, kraw, vraw, kturn, vturn, peak_ref, sum_ref, fade_ref, chunk_max, ahead_ref, outst,
                 wsem, xsem, qsend, qrecv, kvsend, kvrecv, nsend, nrecv, osend, orecv, ksend, krecv, psend, precv, outsem, turnsem,
                 free_sem):
    dp = lax.axis_index("dp")
    me = lax.axis_index("cp")
    chip, core = div(me, 2), rem(me, 2)
    hid = wbuf.shape[1]
    pair = 2 * rows
    new = 8 * rows
    parts = width // TILE
    per_chip = 2 * parts
    tiles = 4 * per_chip
    keys_a = 2 * seg
    keys_b = 2 * seg + new
    coef = math.log2(math.e) * HEAD_DIM ** -0.5
    neg = float("-inf")
    q_tiles = 4 * parts
    p1_tiles = q_tiles + 2
    out_tiles = hid // TILE
    chunk = hid // 4
    turns = 8
    depth = seg // turns

    def device(index):
        return (dp, index)

    partner = flip(me, 1)

    barrier = pltpu.get_barrier_semaphore()
    for rel in range(1, 8):
        pl.semaphore_signal(barrier, inc=1, device_id=device(flip(me, rel)), device_id_type=MESH)

    def remote(src, dst, send, recv, index):
        return pltpu.make_async_remote_copy(
            src_ref=src, dst_ref=dst, send_sem=send, recv_sem=recv, device_id=device(index), device_id_type=MESH)

    my_rows = pl.ds(pl.multiple_of(core * rows, rows), rows)
    other_rows = pl.ds(pl.multiple_of((1 - core) * rows, rows), rows)

    def tile_of(ref, slot, a):
        return ref.at[slot, pl.ds(a * chunk, chunk), :]

    def fetch_kv(ref, n):
        slot = rem(n, WBUFS)
        for a in range(4):
            first = pl.multiple_of((2 * a + core) * HEAD_DIM, HEAD_DIM)
            pltpu.make_async_copy(ref.at[:, pl.ds(first, HEAD_DIM)],
                                  wbuf.at[slot, :, pl.ds(a * HEAD_DIM, HEAD_DIM)], wsem.at[slot, a]).start()

    def fetch_q(n):
        slot = rem(n, WBUFS)
        g, part = div(n - 1, parts), rem(n - 1, parts)
        head = 2 * flip_chip(chip, rem(g + 1, 4)) + core
        first = pl.multiple_of(head * width + part * TILE, TILE)
        for a in range(4):
            pltpu.make_async_copy(wq_in.at[pl.ds(a * chunk, chunk), pl.ds(first, TILE)],
                                  tile_of(wbuf, slot, a), wsem.at[slot, a]).start()

    def fetch_o(m):
        slot = rem(p1_tiles + m, WBUFS)
        first = pl.multiple_of(m * TILE, TILE)
        for a in range(4):
            top = pl.multiple_of((2 * a + core) * width, width)
            pltpu.make_async_copy(wo_in.at[pl.ds(top, width), pl.ds(first, TILE)],
                                  tile_of(wbuf, slot, a), wsem.at[slot, a]).start()

    def wait_tile(n):
        slot = rem(n, WBUFS)
        for a in range(4):
            pltpu.make_async_copy(tile_of(wbuf, slot, a), tile_of(wbuf, slot, a), wsem.at[slot, a]).wait()

    x_local = pltpu.make_async_copy(x_in, hbuf.at[my_rows, :], xsem.at[0])
    x_remote = remote(x_in, hbuf.at[my_rows, :], xsem.at[1], xsem.at[2], partner)
    x_local.start()
    fetch_kv(wk_in, 0)
    pl.semaphore_wait(barrier, 7)
    x_remote.start()
    fetch_q(1)
    fetch_q(2)

    def kv_copy(p, kind):
        peer = flip(me, ORD[p])
        if kind == 0:
            src, dst = kt.at[peer], kbuf.at[pl.ds(p * seg, seg), :]
        else:
            src, dst = vt.at[peer], vbuf.at[:, pl.ds(p * seg, seg)]
        if p == 0:
            return pltpu.make_async_copy(src, dst, kvrecv.at[kind, 0])
        return remote(src, dst, kvsend.at[kind, p], kvrecv.at[kind, p], peer)

    def kv_send(pair_index):
        for p in (2 * pair_index, 2 * pair_index + 1):
            for kind in range(2):
                kv_copy(p, kind).start()

    def kv_wait(p):
        for kind in range(2):
            if p == 0:
                kv_copy(p, kind).wait()
            else:
                kv_copy(p, kind).wait_recv()

    def turn_in(c):
        where = pl.ds(pl.multiple_of(c * depth, depth), depth)
        slot = rem(c, 2)
        return (pltpu.make_async_copy(k_in.at[where], kraw.at[slot], turnsem.at[0, slot]),
                pltpu.make_async_copy(v_in.at[where], vraw.at[slot], turnsem.at[1, slot]))

    def turn_out(c):
        where = pl.ds(pl.multiple_of(c * depth, depth), depth)
        return (pltpu.make_async_copy(kturn, kt.at[:, where, :], turnsem.at[2, 0]),
                pltpu.make_async_copy(vturn, vt.at[:, :, where], turnsem.at[2, 1]))

    def turn(c):
        slot = rem(c, 2)
        acc[pl.ds(0, 8 * depth), :] = kraw[slot].astype(F32).reshape(8 * depth, HEAD_DIM)
        acc[pl.ds(8 * depth, 8 * depth), :] = vraw[slot].astype(F32).reshape(8 * depth, HEAD_DIM)
        for h in range(8):
            kturn[h] = acc[pl.ds(h, depth, stride=8), :].astype(BF16)
            vturn[h] = acc[pl.ds(8 * depth + h, depth, stride=8), :].T.astype(BF16)

    for c in turn_in(0):
        c.start()

    def normalise(first_row):
        def some(i, carry):
            at = pl.multiple_of(first_row + i * 32, 32)
            wide = hbuf[pl.ds(at, 32), :].astype(F32)
            mean_sq = jnp.sum(wide * wide, axis=-1, keepdims=True) * (1.0 / hid)
            hbuf[pl.ds(at, 32), :] = (wide * lax.rsqrt(mean_sq + NORM_EPS) * ln_in[...]).astype(BF16)
            return carry
        lax.fori_loop(0, rows // 32, some, 0)

    x_local.wait()
    normalise(core * rows)
    x_remote.wait_recv()
    normalise((1 - core) * rows)

    def multiply(n):
        slot = rem(n, WBUFS)
        return jnp.dot(hbuf[...], wbuf[slot], preferred_element_type=F32)

    def rotate(e):
        group, part = div(e + parts - 1, parts), rem(e + parts - 1, parts)
        gain = gain_in[jnp.minimum(e, 1)]
        cos_tab, sin_tab = cos_in[...], sin_in[...]
        done = []
        for h in range(HEADS):
            vals = raw[:, h * HEAD_DIM:(h + 1) * HEAD_DIM].astype(F32)
            mean_sq = jnp.sum(vals * vals, axis=-1, keepdims=True) * (1.0 / HEAD_DIM)
            vals = vals * lax.rsqrt(mean_sq + NORM_EPS) * gain
            done.append((vals * cos_tab + pltpu.roll(vals, HEAD_DIM // 2, 1) * sin_tab).astype(BF16))
        done = jnp.concatenate(done, axis=1)
        where = pl.ds(pl.multiple_of(part * TILE, TILE), TILE)
        stage[group, :, where] = done
        qbuf[0, :, where] = done

    def q_copy(rel, part):
        cols = pl.ds(pl.multiple_of(part * TILE, TILE), TILE)
        return remote(stage.at[rel, :, cols], qbuf.at[rel, :, cols], qsend.at[rel, part], qrecv.at[rel, part],
                      2 * flip_chip(chip, rel) + core)

    def new_copy(rel, kind):
        other = flip_chip(chip, rel)
        here = pl.ds(pl.multiple_of(8 * seg + chip * pair, pair), pair)
        if kind == 0:
            first = pl.multiple_of((parts - 1) * TILE + other * HEAD_DIM, HEAD_DIM)
            src, dst = stage.at[0, :, pl.ds(first, HEAD_DIM)], kbuf.at[here, :]
        else:
            src, dst = vstage.at[other], vbuf.at[:, here]
        return remote(src, dst, nsend.at[kind, rel], nrecv.at[kind, rel], 2 * other + core)

    def new_outs(kind):
        copies = []
        for a in range(4):
            if kind == 0:
                src, cols = stage.at[0], pl.ds((parts - 1) * TILE + a * HEAD_DIM, HEAD_DIM)
            else:
                src, cols = raw, pl.ds(a * HEAD_DIM, HEAD_DIM)
            dst = (k_out, v_out)[kind].at[2 * a + core]
            copies.append((
                pltpu.make_async_copy(src.at[my_rows, cols], dst, krecv.at[kind, 0, a]),
                remote(src.at[other_rows, cols], dst, ksend.at[kind, a], krecv.at[kind, 1, a], partner)))
        return copies

    def out_arrival(kind, a):
        dst = (k_out, v_out)[kind].at[2 * a + 1 - core]
        return remote(dst, dst, ksend.at[kind, a], krecv.at[kind, 1, a], partner)

    wait_tile(0)
    raw[...] = multiply(0).astype(BF16)
    fetch_q(3)

    def project(turning, n, carry):
        @pl.when(n == 2)
        def _():
            for rel in range(1, 4):
                new_copy(rel, 0).start()
            for here_copy, there_copy in new_outs(0):
                here_copy.start()
                there_copy.start()

        @pl.when((n >= 3) & (n < 3 + 3 * parts))
        def _():
            e = n - 2
            q_copy(div(e + parts - 1, parts), rem(e + parts - 1, parts)).start()

        if turning:
            @pl.when(n < turns)
            def _():
                for c in turn_in(n):
                    c.start()

            for c in turn_in(n - 1):
                c.wait()

            @pl.when(n >= 2)
            def _():
                for c in turn_out(n - 2):
                    c.wait()
        else:
            @pl.when(n == turns + 1)
            def _():
                for c in turn_out(turns - 1):
                    c.wait()
                for p in range(2):
                    for kind in range(2):
                        kv_copy(p, kind).start()

            @pl.when(n == 3 + 3 * parts)
            def _():
                kv_send(1)

        wait_tile(n)
        rotate(n - 1)
        if turning:
            turn(n - 1)
        raw[...] = multiply(n).astype(BF16)
        if turning:
            for c in turn_out(n - 1):
                c.start()

        @pl.when(n + WBUFS <= q_tiles)
        def _():
            fetch_q(n + WBUFS)

        @pl.when(n + WBUFS == q_tiles + 1)
        def _():
            fetch_kv(wv_in, q_tiles + 1)

        @pl.when((n + WBUFS >= p1_tiles) & (n + WBUFS < p1_tiles + WBUFS - 1))
        def _():
            fetch_o(n + WBUFS - p1_tiles)

        return carry

    lax.fori_loop(1, turns + 1, functools.partial(project, True), 0)
    lax.fori_loop(turns + 1, p1_tiles, functools.partial(project, False), 0)

    here = pl.ds(pl.multiple_of(8 * seg + chip * pair, pair), pair)
    for a in range(4):
        vstage[a] = raw[:, a * HEAD_DIM:(a + 1) * HEAD_DIM].astype(F32).T.astype(BF16)
    kbuf[here, :] = stage[0, :, pl.ds(pl.multiple_of((parts - 1) * TILE + chip * HEAD_DIM, HEAD_DIM), HEAD_DIM)]
    vbuf[:, here] = vstage[chip]

    def acc_rows(t, h):
        return pl.ds(pl.multiple_of((t * HEADS + h) * HEAD_DIM, HEAD_DIM), HEAD_DIM)

    def init(t, carry):
        peak_ref[t] = jnp.full((1, TILE), neg, F32)
        sum_ref[t] = jnp.zeros((1, TILE), F32)
        for h in range(HEADS):
            acc[acc_rows(t, h), :] = jnp.zeros((HEAD_DIM, rows), F32)
        return carry

    lax.fori_loop(0, tiles, init, 0)
    ahead_ref[...] = (lax.broadcasted_iota(jnp.int32, (SUB, rows), 0)
                      - lax.broadcasted_iota(jnp.int32, (SUB, rows), 1))
    for rel in range(1, 4):
        new_copy(rel, 1).start()
    for here_copy, there_copy in new_outs(1):
        here_copy.start()
        there_copy.start()

    def place(t):
        rel, rest = div(t, per_chip), rem(t, per_chip)
        return rel, pl.ds(pl.multiple_of(rem(rest, 2) * rows, rows), rows), div(rest, 2)

    def q_tile(t):
        rel, some_rows, part = place(t)
        block = qbuf[rel, some_rows, pl.ds(pl.multiple_of(part * TILE, TILE), TILE)]
        return jnp.concatenate([block[:, h * HEAD_DIM:(h + 1) * HEAD_DIM] for h in range(HEADS)], axis=0)

    probs = wbuf.at[(p1_tiles + WBUFS - 1) % WBUFS]

    def step(pv=None, sm=None, qk=None, end=None):
        if end is not None:
            finish(end)
        if pv is not None:
            t_pv, base_pv, keys_pv = pv
            fade_pv = fade_ref[...]
        if sm is not None:
            t_sm, keys_sm = sm
            old = peak_ref[t_sm]
            top = jnp.maximum(old, jnp.max(chunk_max[...], axis=0, keepdims=True) * coef)
            fade = jnp.exp2(old - top)
            peak_ref[t_sm] = top
        if qk is not None:
            t_qk, base_qk, keys_qk, has_new = qk
            q = q_tile(t_qk)
            first_row = flip_chip(chip, div(t_qk, per_chip)) * pair + rem(t_qk, 2) * rows if has_new else None
        total = None
        values = None
        peaks = None
        most = max(pv[2] if pv else 0, sm[1] if sm else 0, qk[2] if qk else 0)
        for s in range(most // SUB):
            lines = slice(s * SUB, (s + 1) * SUB)
            if pv is not None and s * SUB < keys_pv:
                v_part = vbuf[:, pl.ds(pl.multiple_of(base_pv + s * SUB, SUB), SUB)]
                o_part = jnp.dot(v_part, probs[lines, :], preferred_element_type=F32)
                values = o_part if values is None else values + o_part
            if sm is not None and s * SUB < keys_sm:
                w = jnp.exp2(scores[lines, :] * coef - top)
                part = jnp.sum(w.reshape(SUB // 8, 8, TILE), axis=0)
                total = part if total is None else total + part
                probs[lines, :] = w.astype(BF16)
            if qk is not None and s * SUB < keys_qk:
                k_part = kbuf[pl.ds(pl.multiple_of(base_qk + s * SUB, SUB), SUB), :]
                sc = lax.dot_general(k_part, q, (((1,), (1,)), ((), ())), preferred_element_type=F32)
                if has_new and s * SUB >= keys_a:
                    seen = ahead_ref[...] <= first_row - (s * SUB - keys_a)
                    sc = jnp.concatenate(
                        [jnp.where(seen, sc[:, h * rows:(h + 1) * rows], neg) for h in range(HEADS)], axis=1)
                scores[lines, :] = sc
                part = jnp.max(sc.reshape(SUB // 8, 8, TILE), axis=0)
                peaks = part if peaks is None else jnp.maximum(peaks, part)
        if qk is not None:
            chunk_max[...] = peaks
        if sm is not None:
            sum_ref[t_sm] = sum_ref[t_sm] * fade + jnp.sum(total, axis=0, keepdims=True)
            fade_ref[...] = fade
        if pv is not None:
            for h in range(HEADS):
                cols = slice(h * rows, (h + 1) * rows)
                acc[acc_rows(t_pv, h), :] = acc[acc_rows(t_pv, h), :] * fade_pv[:, cols] + values[:, cols]

    def finish(t):
        sums = sum_ref[t]
        rel, some_rows, part = place(t)
        done = jnp.concatenate(
            [(acc[acc_rows(t, h), :] / sums[:, h * rows:(h + 1) * rows]).T.astype(BF16) for h in range(HEADS)], axis=1)
        stage[rel, some_rows, pl.ds(pl.multiple_of(part * TILE, TILE), TILE)] = done
        hbuf[some_rows, pl.ds(pl.multiple_of(chip * width + part * TILE, TILE), TILE)] = done

    steps_a = 3 * tiles

    def item_a(i):
        return rem(i, tiles), div(i, tiles) * keys_a, keys_a

    kv_wait(0)
    kv_wait(1)
    step(qk=(*item_a(0), False))
    step(sm=(0, keys_a), qk=(*item_a(1), False))

    def body_a(i, carry):
        nxt = i + 1

        @pl.when((nxt >= per_chip) & (nxt < tiles) & (rem(nxt, 2) == 0))
        def _():
            q_copy(div(nxt, per_chip), div(rem(nxt, per_chip), 2)).wait_recv()

        @pl.when(nxt == 2 * tiles // 3)
        def _():
            kv_send(2)

        @pl.when(nxt == 4 * tiles // 3)
        def _():
            kv_send(3)

        for v in (1, 2):
            @pl.when(nxt == v * tiles)
            def _():
                kv_wait(2 * v)
                kv_wait(2 * v + 1)
        step(pv=item_a(i - 1), sm=(rem(i, tiles), keys_a), qk=(*item_a(nxt), False))
        return carry

    lax.fori_loop(1, steps_a - 1, body_a, 0)

    kv_wait(6)
    kv_wait(7)
    for rel in range(1, 4):
        new_copy(rel, 0).wait_recv()
        new_copy(rel, 1).wait_recv()
        new_copy(rel, 0).wait_send()
        for part in range(parts):
            q_copy(rel, part).wait_send()
    for here_copy, there_copy in new_outs(0):
        here_copy.wait()
        there_copy.wait_send()

    def tile_b(i):
        return (3 - div(i, per_chip)) * per_chip + rem(i, per_chip)

    def o_copy(rel, part):
        cols = pl.ds(pl.multiple_of(part * TILE, TILE), TILE)
        there = pl.ds(pl.multiple_of(chip * width + part * TILE, TILE), TILE)
        return remote(stage.at[rel, :, cols], hbuf.at[:, there], osend.at[rel, part], orecv.at[rel, part],
                      2 * flip_chip(chip, rel) + core)

    def o_arrival(rel, part):
        there = pl.ds(pl.multiple_of(flip_chip(chip, rel) * width + part * TILE, TILE), TILE)
        return remote(hbuf.at[:, there], hbuf.at[:, there], osend.at[rel, part], orecv.at[rel, part],
                      2 * flip_chip(chip, rel) + core)

    base_b = 3 * keys_a

    def item_b(i):
        return tile_b(i), base_b, keys_b

    step(pv=item_a(steps_a - 2), sm=((steps_a - 1) % tiles, keys_a), qk=(*item_b(0), True))
    step(pv=item_a(steps_a - 1), sm=(tile_b(0), keys_b), qk=(*item_b(1), True))
    step(pv=item_b(0), sm=(tile_b(1), keys_b), qk=(*item_b(2), True))

    def body_b(i, carry):
        @pl.when((i >= 4) & (rem(i, 2) == 0) & (i <= 3 * per_chip + 2))
        def _():
            done = i - 4
            o_copy(3 - div(done, per_chip), div(rem(done, per_chip), 2)).start()

        step(pv=item_b(i - 1), sm=(tile_b(i), keys_b), qk=(*item_b(i + 1), True), end=tile_b(i - 2))
        return carry

    lax.fori_loop(2, tiles - 1, body_b, 0)
    step(pv=item_b(tiles - 2), sm=(tile_b(tiles - 1), keys_b), end=tile_b(tiles - 3))
    step(pv=item_b(tiles - 1), end=tile_b(tiles - 2))
    finish(tile_b(tiles - 1))
    fetch_o(WBUFS - 1)

    pl.semaphore_signal(free_sem, inc=1, device_id=device(partner), device_id_type=MESH)
    for rel in range(1, 4):
        for part in range(parts):
            o_arrival(rel, part).wait_recv()
    pl.semaphore_wait(free_sem, 1)

    sent, got, own = 0, out_tiles * rows, 2 * out_tiles * rows

    def lines(first, m):
        return pl.ds(pl.multiple_of(first + m * rows, rows), rows)

    def p_copy(m):
        return remote(scores.at[lines(sent, m), :], scores.at[lines(got, m), :], psend.at[m], precv.at[m], partner)

    def out_copy(m):
        cols = pl.ds(pl.multiple_of(m * TILE, TILE), TILE)
        return pltpu.make_async_copy(outst.at[rem(m, 2)], out.at[:, cols], outsem.at[m])

    def x_copy(m):
        cols = pl.ds(pl.multiple_of(m * TILE, TILE), TILE)
        return pltpu.make_async_copy(x_in.at[:, cols], xres.at[rem(m, 2)], xsem.at[3 + rem(m, 2)])

    def combine(m):
        if isinstance(m, int):
            out_copy(m - 2).wait()
        else:
            @pl.when(m >= 2)
            def _():
                out_copy(m - 2).wait()
        p_copy(m).wait_recv()
        x_copy(m).wait()
        both = scores[lines(own, m), :] + scores[lines(got, m), :]
        outst[rem(m, 2)] = (xres[rem(m, 2)].astype(F32) + both).astype(BF16)
        out_copy(m).start()

    def output(m, carry):
        @pl.when(m >= 1)
        def _():
            p_copy(m - 1).start()

        @pl.when(m >= 2)
        def _():
            combine(m - 2)

        x_copy(m).start()
        wait_tile(p1_tiles + m)
        both = multiply(p1_tiles + m)
        scores[lines(own, m), :] = jnp.where(core == 0, both[:rows], both[rows:])
        scores[lines(sent, m), :] = jnp.where(core == 0, both[rows:], both[:rows])

        @pl.when(m + WBUFS < out_tiles)
        def _():
            fetch_o(m + WBUFS)

        return carry

    lax.fori_loop(0, out_tiles, output, 0)
    p_copy(out_tiles - 1).start()
    combine(out_tiles - 2)
    combine(out_tiles - 1)

    def drain(m, carry):
        p_copy(m).wait_send()
        return carry

    lax.fori_loop(0, out_tiles, drain, 0)
    out_copy(out_tiles - 2).wait()
    out_copy(out_tiles - 1).wait()
    x_remote.wait_send()
    for p in range(1, 8):
        for kind in range(2):
            kv_copy(p, kind).wait_send()
    for rel in range(1, 4):
        new_copy(rel, 1).wait_send()
        for part in range(parts):
            o_copy(rel, part).wait_send()
    for here_copy, there_copy in new_outs(1):
        here_copy.wait()
        there_copy.wait_send()
    for a in range(4):
        out_arrival(0, a).wait_recv()
        out_arrival(1, a).wait_recv()


def block(x, k_cache, v_cache, ln, gains, cos_tab, sin_tab, w_q, w_k, w_v, w_o):
    rows, hid = x.shape
    seg = k_cache.shape[0]
    width = w_q.shape[1] // 8
    pair, new = 2 * rows, 8 * rows
    parts = width // TILE
    tiles = 8 * parts
    out_tiles = hid // TILE
    keys_b = 2 * seg + new
    flops = 4 * (8 * seg + new) * 8 * rows * width + 8 * rows * hid * width * 2
    hbm = pl.BlockSpec(memory_space=pl.ANY)
    vmem = pl.BlockSpec(memory_space=pltpu.VMEM)
    dma = pltpu.SemaphoreType.DMA
    return pl.pallas_call(
        functools.partial(block_kernel, rows, seg, width),
        out_shape=(
            jax.ShapeDtypeStruct((rows, hid), BF16),
            jax.ShapeDtypeStruct((8, rows, HEAD_DIM), BF16),
            jax.ShapeDtypeStruct((8, rows, HEAD_DIM), BF16),
            jax.ShapeDtypeStruct((8, seg, HEAD_DIM), BF16),
            jax.ShapeDtypeStruct((8, HEAD_DIM, seg), BF16),
        ),
        in_specs=[hbm, hbm, hbm, vmem, vmem, vmem, vmem, hbm, hbm, hbm, hbm],
        out_specs=(hbm,) * 5,
        scratch_shapes=[
            pltpu.VMEM((2, rows, TILE), BF16),
            pltpu.VMEM((pair, hid), BF16),
            pltpu.VMEM((WBUFS, hid, TILE), BF16),
            pltpu.VMEM((pair, TILE), BF16),
            pltpu.VMEM((5, pair, width), BF16),
            pltpu.VMEM((4, HEAD_DIM, pair), BF16),
            pltpu.VMEM((4, pair, width), BF16),
            pltpu.VMEM((8 * seg + new, HEAD_DIM), BF16),
            pltpu.VMEM((HEAD_DIM, 8 * seg + new), BF16),
            pltpu.VMEM((max(keys_b, 3 * out_tiles * rows), TILE), F32),
            pltpu.VMEM((tiles * HEADS * HEAD_DIM, rows), F32),
            pltpu.VMEM((2, seg // 8, 8, HEAD_DIM), BF16),
            pltpu.VMEM((2, seg // 8, 8, HEAD_DIM), BF16),
            pltpu.VMEM((8, seg // 8, HEAD_DIM), BF16),
            pltpu.VMEM((8, HEAD_DIM, seg // 8), BF16),
            pltpu.VMEM((tiles, 1, TILE), F32),
            pltpu.VMEM((tiles, 1, TILE), F32),
            pltpu.VMEM((1, TILE), F32),
            pltpu.VMEM((8, TILE), F32),
            pltpu.VMEM((SUB, rows), jnp.int32),
            pltpu.VMEM((2, rows, TILE), BF16),
            dma((WBUFS, 4)),
            dma((5,)),
            dma((4, parts)), dma((4, parts)),
            dma((2, 8)), dma((2, 8)),
            dma((2, 4)), dma((2, 4)),
            dma((4, parts)), dma((4, parts)),
            dma((2, 4)), dma((2, 2, 4)),
            dma((out_tiles,)), dma((out_tiles,)),
            dma((out_tiles,)),
            dma((3, 2)),
            pltpu.SemaphoreType.REGULAR,
        ],
        compiler_params=pltpu.CompilerParams(
            collective_id=0, has_side_effects=True, vmem_limit_bytes=67043328),
        cost_estimate=pl.CostEstimate(flops=flops, bytes_accessed=200 * 1024 * 1024, transcendentals=flops // 512),
        name="block",
    )(x, k_cache, v_cache, ln, gains, cos_tab, sin_tab, w_q, w_k, w_v, w_o)


def solution(mesh):
    cp_size = mesh.shape['cp']
    row_spec = P(('dp', 'cp'), None)
    cache_spec = P(('dp', 'cp'), None, None)
    whole = P()

    def device_step(x_rows, k_cache, v_cache, ln_gain, w_q, w_k, w_v, w_o, q_gain, k_gain):
        rows = x_rows.shape[0]
        prefix_len = k_cache.shape[0] * cp_size
        chip = lax.axis_index('cp') // 2
        positions = (prefix_len + chip * 2 * rows + jnp.arange(2 * rows)).astype(F32)
        half = HEAD_DIM // 2
        inv_freq = ROPE_THETA ** (-jnp.arange(half, dtype=F32) * (2.0 / HEAD_DIM))
        angles = positions[:, None] * inv_freq[None, :]
        cos_half, sin_half = jnp.cos(angles), jnp.sin(angles)
        cos_tab = jnp.concatenate([cos_half, cos_half], axis=1)
        sin_tab = jnp.concatenate([-sin_half, sin_half], axis=1)
        gains = jnp.stack([k_gain, q_gain]).astype(F32)[:, None, :]
        out, k_heads, v_heads, _, _ = block(
            x_rows, k_cache, v_cache, ln_gain.astype(F32)[None, :], gains, cos_tab, sin_tab, w_q, w_k, w_v, w_o)
        return out, jnp.transpose(k_heads, (1, 0, 2)), jnp.transpose(v_heads, (1, 0, 2))

    return jax.shard_map(device_step, mesh=mesh, in_specs=(row_spec, cache_spec, cache_spec, whole, whole, whole, whole, whole, whole, whole), out_specs=(row_spec, cache_spec, cache_spec), check_vma=False)
```

time: 307 us -> 282 us (0.919)
  Pallas kernels: 284 us -> 270 us
  local copies, waits for them, and re-layouts: 18.3 us -> 6.34 us
    pallas_call x1, Pallas kernels: 284 us -> 270 us  [block(): pl.pallas_call(functools.partial(block_kernel, rows, seg, width), out_sha...]
    unnamed x3, local copies, waits for them, and re-layouts: 14 us -> 6.34 us
where the time goes in v3:
time: 282 us; the launch traced here: 281 us
  Pallas kernels  270 us (96%)
  local copies, waits for them, and re-layouts  6.34 us (2%)
  other arithmetic  3.96 us (1%)
    pallas_call x1, Pallas kernels, block(): pl.pallas_call(functools.partial(block_kernel, rows, seg, width), out_sha...  270 us
    unnamed x3, local copies, waits for them, and re-layouts  6.34 us

profile of v3, /device:TPU:0, one launch (start us, length us, event | category | flops | bytes accessed | tf_op | source)
XLA Modules:
  0.0 281.3 jit_solution(11918832707224504769)
XLA Ops:
  0.7 1.3 maximum_convert_fusion.gain_in
  1.9 1.3 broadcast_in_dim.10
  3.2 0.5 fusion
  3.8 0.8 pad_maximum_fusion
  4.6 270.3 %block.1 = (bf16[128,6144]{1,0:T(8,128)(2,1)}, bf16[8,128,128]{2,1,0:T(8,128)(2,1)}, bf16[8,128,128]{2,1,0:T(8,128)(2,1)}, bf16[8,2048,128]{2,1,0:T(8,128)(2,1)}, bf16[8,128,2048]{2,1,0:T(8,128)(2,1)}) custom-call(bf16[128,6144]{1,0:T(8,128)(2,1)} %x_in.1, bf16[2048,8,128]{2,1,0:T(8,128)(2,1)} %k_in.1, bf16[2048,8,128]{2,1,0:T(8,128)(2,1)} %v_in.1, ...), custom_call_target="tpu_custom_call" | custom-call | flops 128849018880 | bytes 209715200 | tf_op jit(solution)/shard_map/block/pallas_call | solution.py:584
  274.9 1.8 copy.13
  276.8 1.8 copy.14
  278.6 2.7 copy.16
  (2 shorter events, 0.0 us)
